TPU v7x, 32 devices: a whole 2x2x4 slice. The times are simulated.
32 devices in a mesh: shift: 2 (over y), expert: 4 (over z), shard: 4 (over x, core).
Axes of the slice: x: 2, y: 2, z: 4, core: 2. Of those that a mesh axis runs over, the one named last changes fastest.
Arguments:
- master_gate: float32 [128, 2048, 1024], P(('shift', 'expert'), 'shard'), parts along dimension 0, may hold values from -0.1875 to 0.1875
- master_up: float32 [128, 2048, 1024], P(('shift', 'expert'), 'shard'), parts along dimension 0, may hold values from -0.1875 to 0.1875
- router_weight: float32 [4096, 64], P(('shift', 'shard'), 'expert'), parts along dimension 0, may hold values from -0.125 to 0.125
- router_gain: float32 [4096], P(('shift', 'shard')), parts along dimension 0, may hold values from 0.25 to 1.75
Outputs:
- final_gate: bfloat16 [128, 2048, 1024], P(('shift', 'expert'), None, 'shard'), parts along dimension 0
- final_up: bfloat16 [128, 2048, 1024], P(('shift', 'expert'), None, 'shard'), parts along dimension 0
- scale_gate: float32 [128, 1024], P(('shift', 'expert'), 'shard'), parts along dimension 0
- scale_up: float32 [128, 1024], P(('shift', 'expert'), 'shard'), parts along dimension 0
- serve_router: bfloat16 [4096, 64], P('shift'), parts along dimension 0
There are 2 independent parts, one for each index of `shift`. A program takes and returns all parts, laid end to end along the dimension named above; each array names one. Nothing has to cross between parts.
All inputs are finite; a program needn't handle non-finite values. Where the computation divides by a largest or mean magnitude, that divisor is 1e-20 or more.
Results may differ from a plain program's by a relative error of at most 0.001.
Values may be sent and summed in bfloat16 or wider, within the bound.
No kernel may reach another device: no remote copies, remote signals or barrier semaphores. Data moves between devices by JAX's collectives and lax.ppermute only.
A program may use at most 256 MiB of HBM per device.

v0:
```python
import jax
import jax.numpy as jnp
from jax import lax
from jax.sharding import PartitionSpec as P


def shards(master_gate, master_up, router_weight, router_gain):
    scale_gate, scale_up = lax.pmax(
        (jnp.max(jnp.abs(master_gate), axis=1), jnp.max(jnp.abs(master_up), axis=1)), "shard"
    )
    narrow_gate, narrow_up = (
        (master_gate / jnp.expand_dims(scale_gate, 1)).astype(jnp.bfloat16),
        (master_up / jnp.expand_dims(scale_up, 1)).astype(jnp.bfloat16),
    )
    final_gate, final_up = (
        lax.all_to_all(narrow_gate, "shard", split_axis=2, concat_axis=1, tiled=True),
        lax.all_to_all(narrow_up, "shard", split_axis=2, concat_axis=1, tiled=True),
    )
    scale_gate = lax.dynamic_slice_in_dim(
        scale_gate, lax.axis_index("shard") * final_gate.shape[2], final_gate.shape[2], axis=1
    )
    scale_up = lax.dynamic_slice_in_dim(
        scale_up, lax.axis_index("shard") * final_up.shape[2], final_up.shape[2], axis=1
    )
    part_router = (router_weight * router_gain[:, None]).astype(jnp.bfloat16)
    row_router = lax.all_gather(part_router, "shard", axis=0, tiled=True)
    serve_router = lax.all_gather(row_router, "expert", axis=1, tiled=True)
    return (final_gate, final_up, scale_gate, scale_up, serve_router)


def solution(mesh):
    in_specs = (
        P(("shift", "expert"), "shard", None),
        P(("shift", "expert"), "shard", None),
        P(("shift", "shard"), "expert"),
        P(("shift", "shard")),
    )
    out_specs = (
        P(("shift", "expert"), None, "shard"),
        P(("shift", "expert"), None, "shard"),
        P(("shift", "expert"), "shard"),
        P(("shift", "expert"), "shard"),
        P("shift", None),
    )
    return jax.shard_map(shards, mesh=mesh, in_specs=in_specs, out_specs=out_specs, check_vma=False)
```

profile of v0, /device:TPU:0, one launch (start us, length us, event | category | flops | bytes accessed | tf_op | source)
XLA Modules:
  0.0 541.3 jit_solution(9778503414393642907)
XLA Ops:
  7.2 0.0 all-reduce.3.cloned.1.call-start
  7.2 0.0 copy-start
  7.2 12.6 %abs_reduce_fusion = f32[16,1024]{1,0:T(8,128)} fusion(f32[16,512,1024]{2,1,0:T(8,128)} %param.5), kind=kLoop, calls=%fused_computation.1 | loop fusion | flops 16760832 | bytes 33619968 | tf_op jit(solution)/shard_map/reduce_max | solution.py:9
  19.8 7.6 %copy-done = f32[16,512,1024]{2,1,0:T(8,128)S(1)} copy-done((f32[16,512,1024]{2,1,0:T(8,128)S(1)}, f32[16,512,1024]{2,1,0:T(8,128)}, u32[]{:S(2)}) %copy-start) | copy-done | bytes 33554456
  27.4 2.7 abs_reduce_fusion.1
  30.1 0.0 all-reduce.3.cloned.1.call-update
  30.2 34.2 %copy.12 = f32[16,512,1024]{1,0,2:T(8,128)} copy(f32[16,512,1024]{2,1,0:T(8,128)} %param.4) | data formatting | bytes 67108864 | tf_op args[0]
  64.4 0.5 all-reduce.3.cloned.1.call-done
  64.9 1.0 copy.11
  66.0 17.7 %divide_convert_fusion.1 = bf16[16,512,1024]{1,0,2:T(8,128)(2,1)} fusion(f32[16,512,1024]{1,0,2:T(8,128)} %copy.12, f32[16,1024]{0,1:T(8,128)S(1)} %copy.11), kind=kLoop, calls=%fused_computation.2 | loop fusion | flops 16777216 | bytes 50397184 | tf_op jit(solution)/shard_map/convert_element_type | solution.py:12
  83.6 7.1 %all-to-all-start = ((bf16[16,512,1024]{1,0,2:T(8,128)(2,1)}), bf16[16,512,1024]{1,0,2:T(8,128)(2,1)}, u32[]{:S(2)}, u32[]{:S(2)}) async-start(bf16[16,512,1024]{1,0,2:T(8,128)(2,1)} %divide_convert_fusion.1), calls=%async_computation | async-start | bytes 33554432 | tf_op jit(solution)/shard_map/all_to_all | solution.py:16
  90.7 0.0 copy-start.1
  90.7 34.2 %copy.15 = f32[16,512,1024]{1,0,2:T(8,128)} copy(f32[16,512,1024]{2,1,0:T(8,128)} %param.5) | data formatting | bytes 67108864 | tf_op args[1]
  124.9 0.0 copy-done.1
  124.9 0.2 copy.14
  125.1 0.0 copy-start.2
  125.1 0.0 copy-start.3
  125.2 17.7 %divide_convert_fusion = bf16[16,512,1024]{1,0,2:T(8,128)(2,1)} fusion(f32[16,512,1024]{1,0,2:T(8,128)} %copy.15, f32[16,1024]{0,1:T(8,128)S(1)} %copy.14), kind=kLoop, calls=%fused_computation | loop fusion | flops 16777216 | bytes 50397184 | tf_op jit(solution)/shard_map/convert_element_type | solution.py:13
  142.8 131.1 %all-to-all-done = bf16[16,512,1024]{1,0,2:T(8,128)(2,1)} async-done(((bf16[16,512,1024]{1,0,2:T(8,128)(2,1)}), bf16[16,512,1024]{1,0,2:T(8,128)(2,1)}, u32[]{:S(2)}, u32[]{:S(2)}) %all-to-all-start) | async-done | bytes 16777248 | tf_op jit(solution)/shard_map/all_to_all | solution.py:16
  273.9 7.0 %all-to-all-start.1 = ((bf16[16,512,1024]{1,0,2:T(8,128)(2,1)}), bf16[16,512,1024]{1,0,2:T(8,128)(2,1)}, u32[]{:S(2)}, u32[]{:S(2)}) async-start(bf16[16,512,1024]{1,0,2:T(8,128)(2,1)} %divide_convert_fusion), calls=%async_computation.1 | async-start | bytes 33554432 | tf_op jit(solution)/shard_map/all_to_all | solution.py:17
  280.9 0.0 copy-done.2
  280.9 0.0 copy-done.3
  280.9 184.1 %all_gather.6 = bf16[2048,16]{0,1:T(8,128)(2,1)S(1)} all-gather(bf16[512,16]{0,1:T(8,128)(2,1)S(1)} %multiply_convert_fusion), channel_id=1, replica_groups=mesh['shift'=2,'expert'=4,'shard'=4] {'shard'}, dimensions={0}, use_global_device_ids=true | all-gather | bytes 81920 | tf_op jit(solution)/shard_map/all_gather | solution.py:26
  465.0 15.1 %all_gather.7 = bf16[2048,64]{0,1:T(8,128)(2,1)S(1)} all-gather(bf16[2048,16]{0,1:T(8,128)(2,1)S(1)} %all_gather.6), channel_id=1, replica_groups=mesh['shift'=2,'expert'=4,'shard'=4] {'expert'}, dimensions={1}, use_global_device_ids=true | all-gather | bytes 327680 | tf_op jit(solution)/shard_map/all_gather | solution.py:27
  480.1 1.3 constant_dynamic-slice_fusion
  481.4 26.2 %copy.13 = bf16[16,4,512,256]{3,2,1,0:T(8,128)(2,1)} copy(bf16[16,4,512,256]{2,0,3,1:T(8,128)(2,1)} %bitcast.1) | data formatting | bytes 33554432 | tf_op jit(solution)/shard_map/all_to_all | solution.py:16
  507.6 0.0 all-to-all-done.1
  507.6 26.2 %copy.16 = bf16[16,4,512,256]{3,2,1,0:T(8,128)(2,1)} copy(bf16[16,4,512,256]{2,0,3,1:T(8,128)(2,1)} %bitcast.4) | data formatting | bytes 33554432 | tf_op jit(solution)/shard_map/all_to_all | solution.py:17
  533.8 0.7 copy.20
  (1 shorter events, 0.0 us)
Async XLA Ops:
  7.2 57.7 %all-reduce.3.cloned.1.call-start = ((), (), s32[]{:S(2)}) async-start(), calls=%async_computation.2 | async-start | bytes 262144 | tf_op jit(solution)/shard_map/pmax | solution.py:8
  7.2 20.2 %copy-start = (f32[16,512,1024]{2,1,0:T(8,128)S(1)}, f32[16,512,1024]{2,1,0:T(8,128)}, u32[]{:S(2)}) copy-start(f32[16,512,1024]{2,1,0:T(8,128)} %param.4) | copy-start | bytes 100663296
  83.6 190.3 %all-to-all-start = ((bf16[16,512,1024]{1,0,2:T(8,128)(2,1)}), bf16[16,512,1024]{1,0,2:T(8,128)(2,1)}, u32[]{:S(2)}, u32[]{:S(2)}) async-start(bf16[16,512,1024]{1,0,2:T(8,128)(2,1)} %divide_convert_fusion.1), calls=%async_computation | async-start | bytes 33554432 | tf_op jit(solution)/shard_map/all_to_all | solution.py:16
  90.7 34.2 %copy-start.1 = (f32[16,1024]{1,0:T(8,128)S(1)}, f32[16,1024]{1,0:T(8,128)}, u32[]{:S(2)}) copy-start(f32[16,1024]{1,0:T(8,128)} %get-tuple-element.6) | copy-start | bytes 196612
  125.1 155.7 %copy-start.2 = (f32[512,16]{0,1:T(8,128)S(1)}, f32[512,16]{0,1:T(8,128)}, u32[]{:S(2)}) copy-start(f32[512,16]{0,1:T(8,128)} %param.6) | copy-start | bytes 98308
  125.1 155.7 %copy-start.3 = (f32[512]{0:T(512)S(1)}, f32[512]{0:T(512)}, u32[]{:S(2)}) copy-start(f32[512]{0:T(512)} %param.7) | copy-start | bytes 6148
  273.9 233.7 %all-to-all-start.1 = ((bf16[16,512,1024]{1,0,2:T(8,128)(2,1)}), bf16[16,512,1024]{1,0,2:T(8,128)(2,1)}, u32[]{:S(2)}, u32[]{:S(2)}) async-start(bf16[16,512,1024]{1,0,2:T(8,128)(2,1)} %divide_convert_fusion), calls=%async_computation.1 | async-start | bytes 33554432 | tf_op jit(solution)/shard_map/all_to_all | solution.py:17
Sparse Core Ops, SparseCore 0:
  30.3 34.5 all-reduce.2
where the time goes:
time: 544 us; the launch traced here: 541 us
  blocking collectives  199 us (37%)
  local copies, waits for them, and re-layouts  132 us (24%)
  waiting for transfers between devices  132 us (24%)
  other arithmetic  50.7 us (9%)
  starting transfers between devices  14.1 us (3%)
  between operations  14.1 us (3%)
    all_gather x1, blocking collectives, shards(): row_router = lax.all_gather(part_router, 'shard', axis=0, tiled=True)  184 us
    all_to_all x1, waiting for transfers between devices, shards(): lax.all_to_all(narrow_gate, 'shard', split_axis=2, concat_axis=1, tiled=T...  131 us
    unnamed x11, local copies, waits for them, and re-layouts  76.7 us
    all_to_all x1, local copies, waits for them, and re-layouts, shards(): lax.all_to_all(narrow_up, 'shard', split_axis=2, concat_axis=1, tiled=True)  26.2 us
    all_to_all x1, local copies, waits for them, and re-layouts, shards(): lax.all_to_all(narrow_gate, 'shard', split_axis=2, concat_axis=1, tiled=T...  26.2 us
    convert_element_type x1, other arithmetic, shards(): (master_gate / jnp.expand_dims(scale_gate, 1)).astype(jnp.bfloat16)  17.7 us
    convert_element_type x1, other arithmetic, shards(): (master_up / jnp.expand_dims(scale_up, 1)).astype(jnp.bfloat16)  17.7 us
    all_gather x1, blocking collectives, shards(): serve_router = lax.all_gather(row_router, 'expert', axis=1, tiled=True)  15.1 us
  transfers between devices with their start and end apart: 3, of which 2 were waited for; matrix products, arithmetic and copies ran while one was open for 21% of the time, Pallas kernels for 0%

commit v1 on v0

v1 whole, which is shorter than its diff:
```python
import functools

import jax
import jax.numpy as jnp
from jax import lax
from jax.experimental import pallas as pl
from jax.experimental.pallas import tpu as pltpu
from jax.sharding import PartitionSpec as P

LANES = 128
PLAN = [(0, 0, 1), (0, 1, 3), (0, 4, 1), (0, 5, 3), (0, 8, 8), (1, 0, 8), (1, 8, 7), (1, 15, 1)]
LEAD = 3
HBM = pl.BlockSpec(memory_space=pl.ANY)


def swap(value, axis, size, step):
    return lax.ppermute(value, axis, [(i, i ^ step) for i in range(size)])


def peak_body(*refs):
    refs[-1][0] = jnp.max(jnp.abs(refs[0][0]), axis=0, keepdims=True)


def peaks(master, first, count, after=()):
    _, rows, cols = master.shape
    return pl.pallas_call(
        peak_body,
        grid=(count,),
        in_specs=[pl.BlockSpec((1, rows, cols), lambda e: (first + e, 0, 0))] + [HBM] * len(after),
        out_specs=pl.BlockSpec((1, 1, cols), lambda e: (e, 0, 0)),
        out_shape=jax.ShapeDtypeStruct((count, 1, cols), jnp.float32),
        name="peaks",
    )(master, *after)


def narrow_body(n, targets, *refs):
    outs = refs[-n:]
    for d in range(n):
        outs[d][0] = (refs[d][0] / refs[n + d][0]).astype(jnp.bfloat16)


def narrow(master, scale, targets, first, count, offset, n, final=None):
    experts, rows, cols = master.shape
    width = cols // n

    def source(d):
        return pl.BlockSpec((1, rows, width), lambda e, t: (first + e, 0, t[d]))

    def scale_of(d):
        return pl.BlockSpec((1, 1, width), lambda e, t: (offset + e, 0, t[d]))

    in_specs = [source(d) for d in range(n)] + [scale_of(d) for d in range(n)]
    args = [master] * n + [scale] * n
    aliases = {}
    if final is not None:
        in_specs.append(HBM)
        args.append(final)
        aliases = {1 + 2 * n: 0}
    piece = jax.ShapeDtypeStruct((count, rows, width), jnp.bfloat16)
    return pl.pallas_call(
        functools.partial(narrow_body, n),
        grid_spec=pltpu.PrefetchScalarGridSpec(
            num_scalar_prefetch=1,
            grid=(count,),
            in_specs=in_specs,
            out_specs=[pl.BlockSpec((1, rows, width), lambda e, t: (first + e, t[0], 0))]
            + [pl.BlockSpec((1, rows, width), lambda e, t: (e, 0, 0)) for _ in range(n - 1)],
        ),
        out_shape=[jax.ShapeDtypeStruct((experts, rows * n, width), jnp.bfloat16)] + [piece] * (n - 1),
        input_output_aliases=aliases,
        name="narrow",
    )(targets, *args)


def spread_direct(value, n):
    got = [swap(value, "shard", n, d) for d in range(n - 1, 0, -1)]
    return functools.reduce(jnp.maximum, got, value)


def spread_doubling(value, n):
    step = 1
    while step < n:
        value = jnp.maximum(value, swap(value, "shard", n, step))
        step *= 2
    return value


def router(weight, gain, n, m):
    part = (weight * gain[:, None]).astype(jnp.bfloat16).T
    experts, rows = part.shape
    mine = lax.axis_index("shard")
    tall = jnp.zeros((experts, rows * n), part.dtype)
    held = part
    step = n // 2
    while step:
        got = swap(held, "shard", n, step)
        held = jnp.concatenate([held, got], axis=1)
        step //= 2
    order = [0]
    step = n // 2
    while step:
        order += [k ^ step for k in order]
        step //= 2
    for k, d in enumerate(order):
        piece = held[:, k * rows : (k + 1) * rows]
        tall = lax.dynamic_update_slice_in_dim(tall, piece, (mine ^ d) * rows, 1)
    mine = lax.axis_index("expert")
    full = jnp.zeros((experts * m, rows * n), part.dtype)
    for d in range(m):
        got = tall if d == 0 else swap(tall, "expert", m, d)
        full = lax.dynamic_update_slice_in_dim(full, got, (mine ^ d) * experts, 0)
    return full.T


def own_columns(scale, n):
    width = scale.shape[1] // n
    return lax.dynamic_slice_in_dim(scale, lax.axis_index("shard") * width, width, axis=1)


def plain(master_gate, master_up, router_weight, router_gain, n):
    scales = lax.pmax(
        (jnp.max(jnp.abs(master_gate), axis=1), jnp.max(jnp.abs(master_up), axis=1)), "shard"
    )
    finals = [
        lax.all_to_all(
            (master / jnp.expand_dims(scale, 1)).astype(jnp.bfloat16), "shard", split_axis=2, concat_axis=1, tiled=True
        )
        for master, scale in zip((master_gate, master_up), scales)
    ]
    part = (router_weight * router_gain[:, None]).astype(jnp.bfloat16)
    part = lax.all_gather(part, "shard", axis=0, tiled=True)
    part = lax.all_gather(part, "expert", axis=1, tiled=True)
    return (*finals, *(own_columns(scale, n) for scale in scales), part)


def shards(n, m, master_gate, master_up, router_weight, router_gain):
    experts, rows, cols = master_gate.shape
    if n & (n - 1) or m & (m - 1) or n == 1 or cols % (n * LANES) or rows % 16 or experts % 16:
        return plain(master_gate, master_up, router_weight, router_gain, n)
    mine = lax.axis_index("shard")
    targets = jnp.stack([mine ^ d for d in range(n)]).astype(jnp.int32)
    masters = (master_gate, master_up)
    unit = experts // 16
    lead = 5 * unit
    plan = [(t, first * unit, count * unit) for t, first, count in PLAN]

    head = spread_direct(peaks(master_gate, 0, lead), n)
    finals = [None, None]
    sent = []
    tail_scales = [None, None]
    for k, (tensor, first, count) in enumerate(plan):
        if k < LEAD:
            scale, offset = head, first
        else:
            scale, offset = tail_scales[tensor], first - (lead if tensor == 0 else 0)
        finals[tensor], *pieces = narrow(masters[tensor], scale, targets, first, count, offset, n, finals[tensor])
        if k == LEAD - 1:
            rest_gate = peaks(master_gate, lead, experts - lead, pieces)
            rest_up = peaks(master_up, 0, experts, pieces)
            rest = spread_doubling(jnp.concatenate([rest_gate, rest_up], axis=0), n)
            tail_scales = [rest[: experts - lead], rest[experts - lead :]]
        sent.append([(d, swap(pieces[d - 1], "shard", n, d)) for d in range(n - 1, 0, -1)])
    for (tensor, first, count), got in zip(plan, sent):
        for d, piece in got[-1:] + got[:-1]:
            finals[tensor] = lax.dynamic_update_slice(finals[tensor], piece, (first, (mine ^ d) * rows, 0))
    scale_gate = jnp.concatenate([head, tail_scales[0]], axis=0)[:, 0]
    scale_up = tail_scales[1][:, 0]
    serve_router = router(router_weight, router_gain, n, m)
    return (*finals, own_columns(scale_gate, n), own_columns(scale_up, n), serve_router)


def solution(mesh):
    in_specs = (
        P(("shift", "expert"), "shard", None),
        P(("shift", "expert"), "shard", None),
        P(("shift", "shard"), "expert"),
        P(("shift", "shard")),
    )
    out_specs = (
        P(("shift", "expert"), None, "shard"),
        P(("shift", "expert"), None, "shard"),
        P(("shift", "expert"), "shard"),
        P(("shift", "expert"), "shard"),
        P("shift", None),
    )
    body = functools.partial(shards, mesh.shape["shard"], mesh.shape["expert"])

    return jax.shard_map(body, mesh=mesh, in_specs=in_specs, out_specs=out_specs, check_vma=False)
```

time: 544 us -> 445 us (0.82)
  blocking collectives: 199 us -> 0 us
  waiting for transfers between devices: 132 us -> 273 us
  Pallas kernels: 0 us -> 88.1 us
  local copies, waits for them, and re-layouts: 132 us -> 46.2 us
  other arithmetic: 50.7 us -> 4.03 us
  starting transfers between devices: 14.1 us -> 31.4 us
  between operations: 14.1 us -> 0.9 us
    ppermute x0 -> x34, waiting for transfers between devices: none -> 273 us  [swap(): return lax.ppermute(value, axis, [(i, i ^ step) for i in range(size)])]
    all_gather x2 -> x0, blocking collectives: 199 us -> none  [the longest x1 184 us: shards(): row_router = lax.all_gather(part_router, 'shard', axis=0, tiled=True)]
    all_to_all x2 -> x0, waiting for transfers between devices: 131 us -> none  [the longest x1 131 us: shards(): lax.all_to_all(narrow_gate, 'shard', split_axis=2, concat_axis=1, tiled=T...]
    pallas_call x0 -> x11, Pallas kernels: none -> 88.1 us  [the longest x8 54.8 us: narrow(): pl.pallas_call(functools.partial(narrow_body, n), grid_spec=pltpu.Prefetc...]
    unnamed x11 -> x46, local copies, waits for them, and re-layouts: 76.7 us -> 2.02 us
    all_to_all x2 -> x0, local copies, waits for them, and re-layouts: 52.3 us -> none  [the longest x1 26.2 us: shards(): lax.all_to_all(narrow_up, 'shard', split_axis=2, concat_axis=1, tiled=True)]
    dynamic_update_slice x0 -> x31, local copies, waits for them, and re-layouts: none -> 41.5 us  [the longest x24 39 us: shards(): lax.dynamic_update_slice(finals[tensor], piece, (first, (mine ^ d) * rows...]
    convert_element_type x3 -> x0, other arithmetic: 35.3 us -> none  [the longest x1 17.7 us: shards(): (master_gate / jnp.expand_dims(scale_gate, 1)).astype(jnp.bfloat16)]
  transfers between devices with their start and end apart: 3 -> 34, of which waited for: 2 -> 12; matrix products, arithmetic and copies ran while one was open for 21% -> 11% of each run, Pallas kernels for 0% -> 19%
where the time goes in v1:
time: 445 us; the launch traced here: 443 us
  waiting for transfers between devices  273 us (61%)
  Pallas kernels  88.1 us (20%)
  local copies, waits for them, and re-layouts  46.2 us (10%)
  starting transfers between devices  31.4 us (7%)
    ppermute x34, waiting for transfers between devices, swap(): return lax.ppermute(value, axis, [(i, i ^ step) for i in range(size)])  273 us
    pallas_call x8, Pallas kernels, narrow(): pl.pallas_call(functools.partial(narrow_body, n), grid_spec=pltpu.Prefetc...  54.8 us
    dynamic_update_slice x24, local copies, waits for them, and re-layouts, shards(): lax.dynamic_update_slice(finals[tensor], piece, (first, (mine ^ d) * rows...  39 us
    pallas_call x3, Pallas kernels, peaks(): pl.pallas_call(peak_body, grid=(count,), in_specs=[pl.BlockSpec((1, rows,...  33.3 us
    ppermute x34, starting transfers between devices, swap(): return lax.ppermute(value, axis, [(i, i ^ step) for i in range(size)])  31.4 us
  transfers between devices with their start and end apart: 34, of which 12 were waited for; matrix products, arithmetic and copies ran while one was open for 11% of the time, Pallas kernels for 19%

profile of v1, /device:TPU:0, one launch (start us, length us, event | category | flops | bytes accessed | tf_op | source)
XLA Modules:
  0.0 443.4 jit_solution(7033687205148587529)
XLA Ops:
  0.7 6.0 %peaks.3 = f32[5,1,1024]{2,1,0:T(1,128)} custom-call(f32[16,512,1024]{2,1,0:T(8,128)} %refs_3_.12), custom_call_target="tpu_custom_call" | custom-call | tf_op jit(solution)/shard_map/peaks/pallas_call | solution.py:26
  7.1 2.5 collective-permute-start.1
  9.7 1.8 collective-permute-start.29
  12.1 1.5 collective-permute-done.29
  15.0 3.2 narrow.8
  18.2 5.8 %narrow.9 = (bf16[16,2048,256]{2,1,0:T(8,128)(2,1)}, bf16[3,512,256]{2,1,0:T(8,128)(2,1)}, bf16[3,512,256]{2,1,0:T(8,128)(2,1)}, bf16[3,512,256]{2,1,0:T(8,128)(2,1)}) custom-call(s32[4]{0:T(128)} %pad_add_fusion.targets, f32[16,512,1024]{2,1,0:T(8,128)} %refs_3_.12, f32[16,512,1024]{2,1,0:T(8,128)} %refs_3_.12, ...), custom_call_target="tpu_custom_call", output_to_operand_aliasing={{0}: (9, {})} | custom-call | tf_op jit(solution)/shard_map/narrow/pallas_call | solution.py:60
  24.0 3.2 narrow.10
  27.2 11.5 %peaks.4 = f32[11,1,1024]{2,1,0:T(1,128)} custom-call(f32[16,512,1024]{2,1,0:T(8,128)} %refs_3_.12, bf16[1,512,256]{2,1,0:T(8,128)(2,1)} %get-tuple-element.39.refs_1_, bf16[1,512,256]{2,1,0:T(8,128)(2,1)} %get-tuple-element.40.refs_2_, bf16[1,512,256]{2,1,0:T(8,128)(2,1)} %get-tuple-element.41.refs_3_), custom_call_target="tpu_custom_call" | custom-call | tf_op jit(solution)/shard_map/peaks/pallas_call | solution.py:26
  38.7 15.8 %peaks.5 = f32[16,1,1024]{2,1,0:T(1,128)} custom-call(f32[16,512,1024]{2,1,0:T(8,128)} %refs_3_.15, bf16[1,512,256]{2,1,0:T(8,128)(2,1)} %get-tuple-element.39.refs_1_, bf16[1,512,256]{2,1,0:T(8,128)(2,1)} %get-tuple-element.40.refs_2_, bf16[1,512,256]{2,1,0:T(8,128)(2,1)} %get-tuple-element.41.refs_3_), custom_call_target="tpu_custom_call" | custom-call | tf_op jit(solution)/shard_map/peaks/pallas_call | solution.py:26
  56.1 1.7 collective-permute-start.6
  58.2 1.9 collective-permute-start.31
  60.0 2.6 collective-permute-start.32
  63.6 1.6 collective-permute-start.4
  65.9 2.5 collective-permute-start.33
  68.4 3.5 collective-permute-done.33
  72.7 1.9 collective-permute-start.12
  74.7 1.6 collective-permute-start.10
  77.0 5.9 %narrow.11 = (bf16[16,2048,256]{2,1,0:T(8,128)(2,1)}, bf16[3,512,256]{2,1,0:T(8,128)(2,1)}, bf16[3,512,256]{2,1,0:T(8,128)(2,1)}, bf16[3,512,256]{2,1,0:T(8,128)(2,1)}) custom-call(s32[4]{0:T(128)} %pad_add_fusion.targets, f32[16,512,1024]{2,1,0:T(8,128)} %refs_3_.12, f32[16,512,1024]{2,1,0:T(8,128)} %refs_3_.12, ...), custom_call_target="tpu_custom_call", output_to_operand_aliasing={{0}: (9, {})} | custom-call | tf_op jit(solution)/shard_map/narrow/pallas_call | solution.py:60
  84.3 11.3 %narrow.13 = (bf16[16,2048,256]{2,1,0:T(8,128)(2,1)}, bf16[8,512,256]{2,1,0:T(8,128)(2,1)}, bf16[8,512,256]{2,1,0:T(8,128)(2,1)}, bf16[8,512,256]{2,1,0:T(8,128)(2,1)}) custom-call(s32[4]{0:T(128)} %pad_add_fusion.targets, f32[16,512,1024]{2,1,0:T(8,128)} %refs_3_.15, f32[16,512,1024]{2,1,0:T(8,128)} %refs_3_.15, f32[16,512,1024]{2,1,0:T(8,128)} %refs_3_.15, ...), custom_call_target="tpu_custom_call" | custom-call | tf_op jit(solution)/shard_map/narrow/pallas_call | solution.py:60
  95.6 25.2 %collective-permute-done.13 = bf16[1,512,256]{2,1,0:T(8,128)(2,1)S(1)} collective-permute-done((bf16[1,512,256]{2,1,0:T(8,128)(2,1)S(1)}, bf16[1,512,256]{2,1,0:T(8,128)(2,1)S(1)}, u32[]{:S(2)}, u32[]{:S(2)}) %collective-permute-start.13) | collective-permute-done | bytes 262176 | tf_op jit(solution)/shard_map/ppermute | solution.py:17
  121.5 10.7 %narrow.14 = (bf16[16,2048,256]{2,1,0:T(8,128)(2,1)}, bf16[7,512,256]{2,1,0:T(8,128)(2,1)}, bf16[7,512,256]{2,1,0:T(8,128)(2,1)}, bf16[7,512,256]{2,1,0:T(8,128)(2,1)}) custom-call(s32[4]{0:T(128)} %pad_add_fusion.targets, f32[16,512,1024]{2,1,0:T(8,128)} %refs_3_.15, f32[16,512,1024]{2,1,0:T(8,128)} %refs_3_.15, ...), custom_call_target="tpu_custom_call", output_to_operand_aliasing={{0}: (9, {})} | custom-call | tf_op jit(solution)/shard_map/narrow/pallas_call | solution.py:60
  134.5 1.6 collective-permute-start.22
  138.2 59.4 %collective-permute-done.15 = bf16[3,512,256]{2,1,0:T(8,128)(2,1)} collective-permute-done((bf16[3,512,256]{2,1,0:T(8,128)(2,1)}, bf16[3,512,256]{2,1,0:T(8,128)(2,1)}, u32[]{:S(2)}, u32[]{:S(2)}) %collective-permute-start.15) | collective-permute-done | bytes 786464 | tf_op jit(solution)/shard_map/ppermute | solution.py:17
  197.6 1.6 collective-permute-start.16
  200.5 11.3 %narrow.12 = (bf16[16,2048,256]{2,1,0:T(8,128)(2,1)}, bf16[8,512,256]{2,1,0:T(8,128)(2,1)}, bf16[8,512,256]{2,1,0:T(8,128)(2,1)}, bf16[8,512,256]{2,1,0:T(8,128)(2,1)}) custom-call(s32[4]{0:T(128)} %pad_add_fusion.targets, f32[16,512,1024]{2,1,0:T(8,128)} %refs_3_.12, f32[16,512,1024]{2,1,0:T(8,128)} %refs_3_.12, ...), custom_call_target="tpu_custom_call", output_to_operand_aliasing={{0}: (9, {})} | custom-call | tf_op jit(solution)/shard_map/narrow/pallas_call | solution.py:60
  211.9 3.4 narrow.15
  218.0 1.7 constant_dynamic-update-slice_fusion.28
  219.7 40.0 %collective-permute-done.16 = bf16[3,512,256]{2,1,0:T(8,128)(2,1)} collective-permute-done((bf16[3,512,256]{2,1,0:T(8,128)(2,1)}, bf16[3,512,256]{2,1,0:T(8,128)(2,1)}, u32[]{:S(2)}, u32[]{:S(2)}) %collective-permute-start.16) | collective-permute-done | bytes 786464 | tf_op jit(solution)/shard_map/ppermute | solution.py:17
  263.5 2.1 constant_dynamic-update-slice_fusion.25
  266.6 2.1 constant_dynamic-update-slice_fusion.24
  268.7 1.7 constant_dynamic-update-slice_fusion.23
  271.0 1.7 constant_dynamic-update-slice_fusion.22
  272.6 1.7 constant_dynamic-update-slice_fusion.21
  274.3 2.1 constant_dynamic-update-slice_fusion.20
  276.4 2.1 constant_dynamic-update-slice_fusion.19
  278.4 2.1 constant_dynamic-update-slice_fusion.18
  280.5 1.5 constant_dynamic-update-slice_fusion.14
  281.9 3.0 constant_dynamic-update-slice_fusion.13
  285.0 3.0 constant_dynamic-update-slice_fusion.12
  288.0 2.8 constant_dynamic-update-slice_fusion.11
  290.9 11.1 %collective-permute-done.24 = bf16[7,512,256]{2,1,0:T(8,128)(2,1)S(1)} collective-permute-done((bf16[7,512,256]{2,1,0:T(8,128)(2,1)}, bf16[7,512,256]{2,1,0:T(8,128)(2,1)S(1)}, u32[]{:S(2)}, u32[]{:S(2)}) %collective-permute-start.24) | collective-permute-done | bytes 1835040 | tf_op jit(solution)/shard_map/ppermute | solution.py:17
  303.6 38.2 %collective-permute-done.25 = bf16[7,512,256]{2,1,0:T(8,128)(2,1)S(1)} collective-permute-done((bf16[7,512,256]{2,1,0:T(8,128)(2,1)}, bf16[7,512,256]{2,1,0:T(8,128)(2,1)S(1)}, u32[]{:S(2)}, u32[]{:S(2)}) %collective-permute-start.25) | collective-permute-done | bytes 1835040 | tf_op jit(solution)/shard_map/ppermute | solution.py:17
  344.5 1.5 constant_dynamic-update-slice_fusion.17
  346.7 39.5 %collective-permute-done.18 = bf16[8,512,256]{2,1,0:T(8,128)(2,1)S(1)} collective-permute-done((bf16[8,512,256]{2,1,0:T(8,128)(2,1)}, bf16[8,512,256]{2,1,0:T(8,128)(2,1)S(1)}, u32[]{:S(2)}, u32[]{:S(2)}) %collective-permute-start.18) | collective-permute-done | bytes 2097184 | tf_op jit(solution)/shard_map/ppermute | solution.py:17
  386.3 1.5 constant_dynamic-update-slice_fusion.16
  387.7 49.1 %collective-permute-done.27 = bf16[1,512,256]{2,1,0:T(8,128)(2,1)S(1)} collective-permute-done((bf16[1,512,256]{2,1,0:T(8,128)(2,1)S(1)}, bf16[1,512,256]{2,1,0:T(8,128)(2,1)S(1)}, u32[]{:S(2)}, u32[]{:S(2)}) %collective-permute-start.27) | collective-permute-done | bytes 262176 | tf_op jit(solution)/shard_map/ppermute | solution.py:17
  437.5 1.5 constant_dynamic-update-slice_fusion.15
  439.0 3.6 collective-permute-done.28
  (121 shorter events, 30.1 us)
Async XLA Ops:
  0.6 9.1 %copy-start.14 = (f32[512,16]{0,1:T(8,128)S(1)}, f32[512,16]{0,1:T(8,128)}, u32[]{:S(2)}) copy-start(f32[512,16]{0,1:T(8,128)} %param.6) | copy-start | bytes 98308
  0.6 9.1 %copy-start.15 = (f32[512]{0:T(512)S(1)}, f32[512]{0:T(512)}, u32[]{:S(2)}) copy-start(f32[512]{0:T(512)} %param.7) | copy-start | bytes 6148
  6.6 7.0 %collective-permute-start.2 = (f32[5,1,1024]{2,1,0:T(1,128)}, f32[5,1,1024]{2,1,0:T(1,128)S(1)}, u32[]{:S(2)}, u32[]{:S(2)}) collective-permute-start(f32[5,1,1024]{2,1,0:T(1,128)} %peaks.3), channel_id=1, source_target_pairs={{0,1},{1,0},{2,3},{3,2},{4,5},{5,4},{6,7},{7,6},{8,9},{9,8},{10,11... | collective-permute-start | bytes 61448 | tf_op jit(solution)/shard_map/ppermute | solution.py:17
  7.1 6.5 %collective-permute-start.1 = (f32[5,1,1024]{2,1,0:T(1,128)}, f32[5,1,1024]{2,1,0:T(1,128)S(1)}, u32[]{:S(2)}, u32[]{:S(2)}) collective-permute-start(f32[5,1,1024]{2,1,0:T(1,128)} %peaks.3), channel_id=1, source_target_pairs={{0,2},{1,3},{2,0},{3,1},{4,6},{5,7},{6,4},{7,5},{8,10},{9,11},{10,... | collective-permute-start | bytes 61448 | tf_op jit(solution)/shard_map/ppermute | solution.py:17
  9.6 4.0 collective-permute-start
  9.7 3.8 collective-permute-start.29
  13.6 44.6 %collective-permute-start.30 = (bf16[16,1024]{1,0:T(8,128)(2,1)S(1)}, bf16[16,1024]{1,0:T(8,128)(2,1)S(1)}, u32[]{:S(2)}, u32[]{:S(2)}) collective-permute-start(bf16[16,1024]{1,0:T(8,128)(2,1)S(1)} %pad_maximum_fusion.1), channel_id=1, source_target_pairs={{0,1},{1,0},{2,3},{3,2},{4,5},{5,4},{6,7},{7,6},{8,9},{9,8},{10,11... | collective-permute-start | bytes 98312 | tf_op jit(solution)/shard_map/ppermute | solution.py:17
  38.6 15.9 %copy-start.5 = (f32[11,1,1024]{2,1,0:T(1,128)S(1)}, f32[11,1,1024]{2,1,0:T(1,128)}, u32[]{:S(2)}) copy-start(f32[11,1,1024]{2,1,0:T(1,128)} %peaks.4) | copy-start | bytes 135172
  38.6 17.4 %copy-start.21 = (bf16[1,512,256]{2,1,0:T(8,128)(2,1)S(1)}, bf16[1,512,256]{2,1,0:T(8,128)(2,1)}, u32[]{:S(2)}) copy-start(bf16[1,512,256]{2,1,0:T(8,128)(2,1)} %get-tuple-element.45) | copy-start | bytes 786436
  38.6 17.5 %copy-start.20 = (bf16[1,512,256]{2,1,0:T(8,128)(2,1)S(1)}, bf16[1,512,256]{2,1,0:T(8,128)(2,1)}, u32[]{:S(2)}) copy-start(bf16[1,512,256]{2,1,0:T(8,128)(2,1)} %get-tuple-element.46) | copy-start | bytes 786436
  38.7 19.2 %copy-start.19 = (bf16[1,512,256]{2,1,0:T(8,128)(2,1)S(1)}, bf16[1,512,256]{2,1,0:T(8,128)(2,1)}, u32[]{:S(2)}) copy-start(bf16[1,512,256]{2,1,0:T(8,128)(2,1)} %get-tuple-element.47) | copy-start | bytes 786436
  38.7 33.3 %copy-start.4 = (bf16[1,512,256]{2,1,0:T(8,128)(2,1)S(1)}, bf16[1,512,256]{2,1,0:T(8,128)(2,1)}, u32[]{:S(2)}) copy-start(bf16[1,512,256]{2,1,0:T(8,128)(2,1)} %get-tuple-element.39.refs_1_) | copy-start | bytes 786436
  38.7 34.0 %copy-start.3 = (bf16[1,512,256]{2,1,0:T(8,128)(2,1)S(1)}, bf16[1,512,256]{2,1,0:T(8,128)(2,1)}, u32[]{:S(2)}) copy-start(bf16[1,512,256]{2,1,0:T(8,128)(2,1)} %get-tuple-element.41.refs_3_) | copy-start | bytes 786436
  55.5 4.6 %collective-permute-start.3 = (f32[27,1,1024]{2,1,0:T(1,128)S(1)}, f32[27,1,1024]{2,1,0:T(1,128)S(1)}, u32[]{:S(2)}, u32[]{:S(2)}) collective-permute-start(f32[27,1,1024]{2,1,0:T(1,128)S(1)} %pad_maximum_fusion), channel_id=1, source_target_pairs={{0,1},{1,0},{2,3},{3,2},{4,5},{5,4},{6,7},{7,6},{8,9},{9,8},{10,11... | collective-permute-start | bytes 331784 | tf_op jit(solution)/shard_map/ppermute | solution.py:17
  56.0 16.7 %collective-permute-start.5 = (bf16[1,512,256]{2,1,0:T(8,128)(2,1)S(1)}, bf16[1,512,256]{2,1,0:T(8,128)(2,1)S(1)}, u32[]{:S(2)}, u32[]{:S(2)}) collective-permute-start(bf16[1,512,256]{2,1,0:T(8,128)(2,1)S(1)} %copy-done.21), channel_id=1, source_target_pairs={{0,1},{1,0},{2,3},{3,2},{4,5},{5,4},{6,7},{7,6},{8,9},{9,8},{10,11... | collective-permute-start | bytes 786440 | tf_op jit(solution)/shard_map/ppermute | solution.py:17
  56.1 18.5 %collective-permute-start.6 = (bf16[1,512,256]{2,1,0:T(8,128)(2,1)S(1)}, bf16[1,512,256]{2,1,0:T(8,128)(2,1)S(1)}, u32[]{:S(2)}, u32[]{:S(2)}) collective-permute-start(bf16[1,512,256]{2,1,0:T(8,128)(2,1)S(1)} %copy-done.20), channel_id=1, source_target_pairs={{0,3},{1,2},{2,1},{3,0},{4,7},{5,6},{6,5},{7,4},{8,11},{9,10},{10,... | collective-permute-start | bytes 786440 | tf_op jit(solution)/shard_map/ppermute | solution.py:17
  57.8 16.8 %collective-permute-start.7 = (bf16[1,512,256]{2,1,0:T(8,128)(2,1)S(1)}, bf16[1,512,256]{2,1,0:T(8,128)(2,1)S(1)}, u32[]{:S(2)}, u32[]{:S(2)}) collective-permute-start(bf16[1,512,256]{2,1,0:T(8,128)(2,1)S(1)} %copy-done.19), channel_id=1, source_target_pairs={{0,2},{1,3},{2,0},{3,1},{4,6},{5,7},{6,4},{7,5},{8,10},{9,11},{10,... | collective-permute-start | bytes 786440 | tf_op jit(solution)/shard_map/ppermute | solution.py:17
  58.2 5.4 %collective-permute-start.31 = (bf16[16,2048]{1,0:T(8,128)(2,1)S(1)}, bf16[16,2048]{1,0:T(8,128)(2,1)S(1)}, u32[]{:S(2)}, u32[]{:S(2)}) collective-permute-start(bf16[16,2048]{1,0:T(8,128)(2,1)S(1)} %slice_dynamic-update-slice_fusion), channel_id=1, source_target_pairs={{0,4},{4,0},{8,12},{12,8},{1,5},{5,1},{9,13},{13,9},{2,6},{6,2},{1... | collective-permute-start | bytes 196616 | tf_op jit(solution)/shard_map/ppermute | solution.py:17
  60.0 5.9 %collective-permute-start.32 = (bf16[16,2048]{1,0:T(8,128)(2,1)S(1)}, bf16[16,2048]{1,0:T(8,128)(2,1)S(1)}, u32[]{:S(2)}, u32[]{:S(2)}) collective-permute-start(bf16[16,2048]{1,0:T(8,128)(2,1)S(1)} %slice_dynamic-update-slice_fusion), channel_id=1, source_target_pairs={{0,8},{4,12},{8,0},{12,4},{1,9},{5,13},{9,1},{13,5},{2,10},{6,14},... | collective-permute-start | bytes 196616 | tf_op jit(solution)/shard_map/ppermute | solution.py:17
  63.6 9.1 %collective-permute-start.4 = (f32[27,1,1024]{2,1,0:T(1,128)S(1)}, f32[27,1,1024]{2,1,0:T(1,128)S(1)}, u32[]{:S(2)}, u32[]{:S(2)}) collective-permute-start(f32[27,1,1024]{2,1,0:T(1,128)S(1)} %fusion.2), channel_id=1, source_target_pairs={{0,2},{1,3},{2,0},{3,1},{4,6},{5,7},{6,4},{7,5},{8,10},{9,11},{10,... | collective-permute-start | bytes 331784 | tf_op jit(solution)/shard_map/ppermute | solution.py:17
  65.9 6.1 %collective-permute-start.33 = (bf16[16,2048]{1,0:T(8,128)(2,1)S(1)}, bf16[16,2048]{1,0:T(8,128)(2,1)S(1)}, u32[]{:S(2)}, u32[]{:S(2)}) collective-permute-start(bf16[16,2048]{1,0:T(8,128)(2,1)S(1)} %slice_dynamic-update-slice_fusion), channel_id=1, source_target_pairs={{0,12},{4,8},{8,4},{12,0},{1,13},{5,9},{9,5},{13,1},{2,14},{6,10},... | collective-permute-start | bytes 196616 | tf_op jit(solution)/shard_map/ppermute | solution.py:17
  72.0 11.0 %collective-permute-start.11 = (bf16[1,512,256]{2,1,0:T(8,128)(2,1)S(1)}, bf16[1,512,256]{2,1,0:T(8,128)(2,1)S(1)}, u32[]{:S(2)}, u32[]{:S(2)}) collective-permute-start(bf16[1,512,256]{2,1,0:T(8,128)(2,1)S(1)} %copy-done.4), channel_id=1, source_target_pairs={{0,1},{1,0},{2,3},{3,2},{4,5},{5,4},{6,7},{7,6},{8,9},{9,8},{10,11... | collective-permute-start | bytes 786440 | tf_op jit(solution)/shard_map/ppermute | solution.py:17
  72.7 59.5 %collective-permute-start.8 = (bf16[3,512,256]{2,1,0:T(8,128)(2,1)}, bf16[3,512,256]{2,1,0:T(8,128)(2,1)S(1)}, u32[]{:S(2)}, u32[]{:S(2)}) collective-permute-start(bf16[3,512,256]{2,1,0:T(8,128)(2,1)} %get-tuple-element.48), channel_id=1, source_target_pairs={{0,1},{1,0},{2,3},{3,2},{4,5},{5,4},{6,7},{7,6},{8,9},{9,8},{10,11... | collective-permute-start | bytes 2359304 | tf_op jit(solution)/shard_map/ppermute | solution.py:17
  72.7 10.5 %collective-permute-start.12 = (bf16[1,512,256]{2,1,0:T(8,128)(2,1)S(1)}, bf16[1,512,256]{2,1,0:T(8,128)(2,1)S(1)}, u32[]{:S(2)}, u32[]{:S(2)}) collective-permute-start(bf16[1,512,256]{2,1,0:T(8,128)(2,1)S(1)} %copy-done.3), channel_id=1, source_target_pairs={{0,3},{1,2},{2,1},{3,0},{4,7},{5,6},{6,5},{7,4},{8,11},{9,10},{10,... | collective-permute-start | bytes 786440 | tf_op jit(solution)/shard_map/ppermute | solution.py:17
  74.6 58.2 %collective-permute-start.9 = (bf16[3,512,256]{2,1,0:T(8,128)(2,1)}, bf16[3,512,256]{2,1,0:T(8,128)(2,1)}, u32[]{:S(2)}, u32[]{:S(2)}) collective-permute-start(bf16[3,512,256]{2,1,0:T(8,128)(2,1)} %get-tuple-element.49), channel_id=1, source_target_pairs={{0,3},{1,2},{2,1},{3,0},{4,7},{5,6},{6,5},{7,4},{8,11},{9,10},{10,... | collective-permute-start | bytes 2359304 | tf_op jit(solution)/shard_map/ppermute | solution.py:17
  74.7 59.4 %collective-permute-start.10 = (bf16[3,512,256]{2,1,0:T(8,128)(2,1)}, bf16[3,512,256]{2,1,0:T(8,128)(2,1)}, u32[]{:S(2)}, u32[]{:S(2)}) collective-permute-start(bf16[3,512,256]{2,1,0:T(8,128)(2,1)} %get-tuple-element.50), channel_id=1, source_target_pairs={{0,2},{1,3},{2,0},{3,1},{4,6},{5,7},{6,4},{7,5},{8,10},{9,11},{10,... | collective-permute-start | bytes 2359304 | tf_op jit(solution)/shard_map/ppermute | solution.py:17
  83.0 12.6 %copy-start.11 = (bf16[1,512,256]{2,1,0:T(8,128)(2,1)}, bf16[1,512,256]{2,1,0:T(8,128)(2,1)S(1)}, u32[]{:S(2)}) copy-start(bf16[1,512,256]{2,1,0:T(8,128)(2,1)S(1)} %collective-permute-done.11) | copy-start | bytes 786436
  83.0 51.6 %collective-permute-start.14 = (bf16[3,512,256]{2,1,0:T(8,128)(2,1)}, bf16[3,512,256]{2,1,0:T(8,128)(2,1)}, u32[]{:S(2)}, u32[]{:S(2)}) collective-permute-start(bf16[3,512,256]{2,1,0:T(8,128)(2,1)} %get-tuple-element.51), channel_id=1, source_target_pairs={{0,1},{1,0},{2,3},{3,2},{4,5},{5,4},{6,7},{7,6},{8,9},{9,8},{10,11... | collective-permute-start | bytes 2359304 | tf_op jit(solution)/shard_map/ppermute | solution.py:17
  83.2 12.3 %copy-start.12 = (bf16[1,512,256]{2,1,0:T(8,128)(2,1)}, bf16[1,512,256]{2,1,0:T(8,128)(2,1)S(1)}, u32[]{:S(2)}) copy-start(bf16[1,512,256]{2,1,0:T(8,128)(2,1)S(1)} %collective-permute-done.12) | copy-start | bytes 786436
  83.2 37.5 %collective-permute-start.13 = (bf16[1,512,256]{2,1,0:T(8,128)(2,1)S(1)}, bf16[1,512,256]{2,1,0:T(8,128)(2,1)S(1)}, u32[]{:S(2)}, u32[]{:S(2)}) collective-permute-start(bf16[1,512,256]{2,1,0:T(8,128)(2,1)S(1)} %copy-done.2), channel_id=1, source_target_pairs={{0,2},{1,3},{2,0},{3,1},{4,6},{5,7},{6,4},{7,5},{8,10},{9,11},{10,... | collective-permute-start | bytes 786440 | tf_op jit(solution)/shard_map/ppermute | solution.py:17
  121.5 140.7 %collective-permute-start.20 = (bf16[8,512,256]{2,1,0:T(8,128)(2,1)}, bf16[8,512,256]{2,1,0:T(8,128)(2,1)S(1)}, u32[]{:S(2)}, u32[]{:S(2)}) collective-permute-start(bf16[8,512,256]{2,1,0:T(8,128)(2,1)} %get-tuple-element.60), channel_id=1, source_target_pairs={{0,1},{1,0},{2,3},{3,2},{4,5},{5,4},{6,7},{7,6},{8,9},{9,8},{10,11... | collective-permute-start | bytes 6291464 | tf_op jit(solution)/shard_map/ppermute | solution.py:17
  132.2 129.3 %collective-permute-start.23 = (bf16[7,512,256]{2,1,0:T(8,128)(2,1)}, bf16[7,512,256]{2,1,0:T(8,128)(2,1)}, u32[]{:S(2)}, u32[]{:S(2)}) collective-permute-start(bf16[7,512,256]{2,1,0:T(8,128)(2,1)} %get-tuple-element.63), channel_id=1, source_target_pairs={{0,1},{1,0},{2,3},{3,2},{4,5},{5,4},{6,7},{7,6},{8,9},{9,8},{10,11... | collective-permute-start | bytes 5505032 | tf_op jit(solution)/shard_map/ppermute | solution.py:17
  132.8 132.8 %collective-permute-start.21 = (bf16[8,512,256]{2,1,0:T(8,128)(2,1)}, bf16[8,512,256]{2,1,0:T(8,128)(2,1)}, u32[]{:S(2)}, u32[]{:S(2)}) collective-permute-start(bf16[8,512,256]{2,1,0:T(8,128)(2,1)} %get-tuple-element.61), channel_id=1, source_target_pairs={{0,3},{1,2},{2,1},{3,0},{4,7},{5,6},{6,5},{7,4},{8,11},{9,10},{10,... | collective-permute-start | bytes 6291464 | tf_op jit(solution)/shard_map/ppermute | solution.py:17
  134.1 63.5 %collective-permute-start.15 = (bf16[3,512,256]{2,1,0:T(8,128)(2,1)}, bf16[3,512,256]{2,1,0:T(8,128)(2,1)}, u32[]{:S(2)}, u32[]{:S(2)}) collective-permute-start(bf16[3,512,256]{2,1,0:T(8,128)(2,1)} %get-tuple-element.52), channel_id=1, source_target_pairs={{0,3},{1,2},{2,1},{3,0},{4,7},{5,6},{6,5},{7,4},{8,11},{9,10},{10,... | collective-permute-start | bytes 2359304 | tf_op jit(solution)/shard_map/ppermute | solution.py:17
  134.5 135.8 %collective-permute-start.22 = (bf16[8,512,256]{2,1,0:T(8,128)(2,1)}, bf16[8,512,256]{2,1,0:T(8,128)(2,1)}, u32[]{:S(2)}, u32[]{:S(2)}) collective-permute-start(bf16[8,512,256]{2,1,0:T(8,128)(2,1)} %get-tuple-element.62), channel_id=1, source_target_pairs={{0,2},{1,3},{2,0},{3,1},{4,6},{5,7},{6,4},{7,5},{8,10},{9,11},{10,... | collective-permute-start | bytes 6291464 | tf_op jit(solution)/shard_map/ppermute | solution.py:17
  197.6 62.1 %collective-permute-start.16 = (bf16[3,512,256]{2,1,0:T(8,128)(2,1)}, bf16[3,512,256]{2,1,0:T(8,128)(2,1)}, u32[]{:S(2)}, u32[]{:S(2)}) collective-permute-start(bf16[3,512,256]{2,1,0:T(8,128)(2,1)} %get-tuple-element.53), channel_id=1, source_target_pairs={{0,2},{1,3},{2,0},{3,1},{4,6},{5,7},{6,4},{7,5},{8,10},{9,11},{10,... | collective-permute-start | bytes 2359304 | tf_op jit(solution)/shard_map/ppermute | solution.py:17
  211.9 48.9 %copy-start.7 = (bf16[1,512,256]{2,1,0:T(8,128)(2,1)S(1)}, bf16[1,512,256]{2,1,0:T(8,128)(2,1)}, u32[]{:S(2)}) copy-start(bf16[1,512,256]{2,1,0:T(8,128)(2,1)} %copy-done.6) | copy-start | bytes 786436
  215.3 86.7 %copy-start.18 = (bf16[1,512,256]{2,1,0:T(8,128)(2,1)S(1)}, bf16[1,512,256]{2,1,0:T(8,128)(2,1)}, u32[]{:S(2)}) copy-start(bf16[1,512,256]{2,1,0:T(8,128)(2,1)} %get-tuple-element.66) | copy-start | bytes 786436
  215.3 126.4 %copy-start.17 = (bf16[1,512,256]{2,1,0:T(8,128)(2,1)S(1)}, bf16[1,512,256]{2,1,0:T(8,128)(2,1)}, u32[]{:S(2)}) copy-start(bf16[1,512,256]{2,1,0:T(8,128)(2,1)} %get-tuple-element.67) | copy-start | bytes 786436
  259.7 42.3 %collective-permute-start.24 = (bf16[7,512,256]{2,1,0:T(8,128)(2,1)}, bf16[7,512,256]{2,1,0:T(8,128)(2,1)S(1)}, u32[]{:S(2)}, u32[]{:S(2)}) collective-permute-start(bf16[7,512,256]{2,1,0:T(8,128)(2,1)} %get-tuple-element.64), channel_id=1, source_target_pairs={{0,3},{1,2},{2,1},{3,0},{4,7},{5,6},{6,5},{7,4},{8,11},{9,10},{10,... | collective-permute-start | bytes 5505032 | tf_op jit(solution)/shard_map/ppermute | solution.py:17
  261.5 82.7 %collective-permute-start.17 = (bf16[8,512,256]{2,1,0:T(8,128)(2,1)}, bf16[8,512,256]{2,1,0:T(8,128)(2,1)S(1)}, u32[]{:S(2)}, u32[]{:S(2)}) collective-permute-start(bf16[8,512,256]{2,1,0:T(8,128)(2,1)} %get-tuple-element.54), channel_id=1, source_target_pairs={{0,1},{1,0},{2,3},{3,2},{4,5},{5,4},{6,7},{7,6},{8,9},{9,8},{10,11... | collective-permute-start | bytes 6291464 | tf_op jit(solution)/shard_map/ppermute | solution.py:17
  262.2 79.5 %collective-permute-start.25 = (bf16[7,512,256]{2,1,0:T(8,128)(2,1)}, bf16[7,512,256]{2,1,0:T(8,128)(2,1)S(1)}, u32[]{:S(2)}, u32[]{:S(2)}) collective-permute-start(bf16[7,512,256]{2,1,0:T(8,128)(2,1)} %get-tuple-element.65), channel_id=1, source_target_pairs={{0,2},{1,3},{2,0},{3,1},{4,6},{5,7},{6,4},{7,5},{8,10},{9,11},{10,... | collective-permute-start | bytes 5505032 | tf_op jit(solution)/shard_map/ppermute | solution.py:17
  263.5 80.7 %copy-start.16 = (bf16[1,512,256]{2,1,0:T(8,128)(2,1)S(1)}, bf16[1,512,256]{2,1,0:T(8,128)(2,1)}, u32[]{:S(2)}) copy-start(bf16[1,512,256]{2,1,0:T(8,128)(2,1)} %get-tuple-element.68) | copy-start | bytes 786436
  265.6 120.7 %collective-permute-start.18 = (bf16[8,512,256]{2,1,0:T(8,128)(2,1)}, bf16[8,512,256]{2,1,0:T(8,128)(2,1)S(1)}, u32[]{:S(2)}, u32[]{:S(2)}) collective-permute-start(bf16[8,512,256]{2,1,0:T(8,128)(2,1)} %get-tuple-element.55), channel_id=1, source_target_pairs={{0,3},{1,2},{2,1},{3,0},{4,7},{5,6},{6,5},{7,4},{8,11},{9,10},{10,... | collective-permute-start | bytes 6291464 | tf_op jit(solution)/shard_map/ppermute | solution.py:17
  270.4 167.2 %collective-permute-start.19 = (bf16[8,512,256]{2,1,0:T(8,128)(2,1)}, bf16[8,512,256]{2,1,0:T(8,128)(2,1)S(1)}, u32[]{:S(2)}, u32[]{:S(2)}) collective-permute-start(bf16[8,512,256]{2,1,0:T(8,128)(2,1)} %get-tuple-element.56), channel_id=1, source_target_pairs={{0,2},{1,3},{2,0},{3,1},{4,6},{5,7},{6,4},{7,5},{8,10},{9,11},{10,... | collective-permute-start | bytes 6291464 | tf_op jit(solution)/shard_map/ppermute | solution.py:17
  302.0 44.0 %collective-permute-start.26 = (bf16[1,512,256]{2,1,0:T(8,128)(2,1)S(1)}, bf16[1,512,256]{2,1,0:T(8,128)(2,1)S(1)}, u32[]{:S(2)}, u32[]{:S(2)}) collective-permute-start(bf16[1,512,256]{2,1,0:T(8,128)(2,1)S(1)} %copy-done.18), channel_id=1, source_target_pairs={{0,1},{1,0},{2,3},{3,2},{4,5},{5,4},{6,7},{7,6},{8,9},{9,8},{10,11... | collective-permute-start | bytes 786440 | tf_op jit(solution)/shard_map/ppermute | solution.py:17
  341.7 95.1 %collective-permute-start.27 = (bf16[1,512,256]{2,1,0:T(8,128)(2,1)S(1)}, bf16[1,512,256]{2,1,0:T(8,128)(2,1)S(1)}, u32[]{:S(2)}, u32[]{:S(2)}) collective-permute-start(bf16[1,512,256]{2,1,0:T(8,128)(2,1)S(1)} %copy-done.17), channel_id=1, source_target_pairs={{0,3},{1,2},{2,1},{3,0},{4,7},{5,6},{6,5},{7,4},{8,11},{9,10},{10,... | collective-permute-start | bytes 786440 | tf_op jit(solution)/shard_map/ppermute | solution.py:17
  344.2 98.4 %collective-permute-start.28 = (bf16[1,512,256]{2,1,0:T(8,128)(2,1)S(1)}, bf16[1,512,256]{2,1,0:T(8,128)(2,1)S(1)}, u32[]{:S(2)}, u32[]{:S(2)}) collective-permute-start(bf16[1,512,256]{2,1,0:T(8,128)(2,1)S(1)} %copy-done.16), channel_id=1, source_target_pairs={{0,2},{1,3},{2,0},{3,1},{4,6},{5,7},{6,4},{7,5},{8,10},{9,11},{10,... | collective-permute-start | bytes 786440 | tf_op jit(solution)/shard_map/ppermute | solution.py:17
  (8 other events, 28.1 us)

commit v2 on v1

--- a/solution.py
+++ b/solution.py
@@ -8,7 +8,7 @@
 from jax.sharding import PartitionSpec as P
 
 LANES = 128
-PLAN = [(0, 0, 1), (0, 1, 3), (0, 4, 1), (0, 5, 3), (0, 8, 8), (1, 0, 8), (1, 8, 7), (1, 15, 1)]
+PLAN = [(0, 0, 1), (0, 1, 2), (0, 3, 1), (0, 4, 3), (0, 7, 9), (1, 0, 8), (1, 8, 7), (1, 15, 1)]
 LEAD = 3
 HBM = pl.BlockSpec(memory_space=pl.ANY)
 
@@ -18,16 +18,17 @@
 
 
 def peak_body(*refs):
-    refs[-1][0] = jnp.max(jnp.abs(refs[0][0]), axis=0, keepdims=True)
+    refs[-1][...] = jnp.max(jnp.abs(refs[0][...]), axis=1, keepdims=True)
 
 
 def peaks(master, first, count, after=()):
     _, rows, cols = master.shape
+    group = 2 if first % 2 == 0 and count % 2 == 0 else 1
     return pl.pallas_call(
         peak_body,
-        grid=(count,),
-        in_specs=[pl.BlockSpec((1, rows, cols), lambda e: (first + e, 0, 0))] + [HBM] * len(after),
-        out_specs=pl.BlockSpec((1, 1, cols), lambda e: (e, 0, 0)),
+        grid=(count // group,),
+        in_specs=[pl.BlockSpec((group, rows, cols), lambda e: (first // group + e, 0, 0))] + [HBM] * len(after),
+        out_specs=pl.BlockSpec((group, 1, cols), lambda e: (e, 0, 0)),
         out_shape=jax.ShapeDtypeStruct((count, 1, cols), jnp.float32),
         name="peaks",
     )(master, *after)
@@ -39,15 +40,16 @@
         outs[d][0] = (refs[d][0] / refs[n + d][0]).astype(jnp.bfloat16)
 
 
-def narrow(master, scale, targets, first, count, offset, n, final=None):
+def narrow(master, scale, targets, first, count, offset, n, cuts, final=None):
     experts, rows, cols = master.shape
     width = cols // n
+    block = (1, rows // cuts, width)
 
     def source(d):
-        return pl.BlockSpec((1, rows, width), lambda e, t: (first + e, 0, t[d]))
+        return pl.BlockSpec(block, lambda e, r, t: (first + e, r, t[d]))
 
     def scale_of(d):
-        return pl.BlockSpec((1, 1, width), lambda e, t: (offset + e, 0, t[d]))
+        return pl.BlockSpec((1, 1, width), lambda e, r, t: (offset + e, 0, t[d]))
 
     in_specs = [source(d) for d in range(n)] + [scale_of(d) for d in range(n)]
     args = [master] * n + [scale] * n
@@ -61,10 +63,10 @@
         functools.partial(narrow_body, n),
         grid_spec=pltpu.PrefetchScalarGridSpec(
             num_scalar_prefetch=1,
-            grid=(count,),
+            grid=(count, cuts),
             in_specs=in_specs,
-            out_specs=[pl.BlockSpec((1, rows, width), lambda e, t: (first + e, t[0], 0))]
-            + [pl.BlockSpec((1, rows, width), lambda e, t: (e, 0, 0)) for _ in range(n - 1)],
+            out_specs=[pl.BlockSpec(block, lambda e, r, t: (first + e, t[0] * cuts + r, 0))]
+            + [pl.BlockSpec(block, lambda e, r, t: (e, r, 0)) for _ in range(n - 1)],
         ),
         out_shape=[jax.ShapeDtypeStruct((experts, rows * n, width), jnp.bfloat16)] + [piece] * (n - 1),
         input_output_aliases=aliases,
@@ -135,13 +137,13 @@
 
 def shards(n, m, master_gate, master_up, router_weight, router_gain):
     experts, rows, cols = master_gate.shape
-    if n & (n - 1) or m & (m - 1) or n == 1 or cols % (n * LANES) or rows % 16 or experts % 16:
+    if n & (n - 1) or m & (m - 1) or n == 1 or cols % (n * LANES) or rows % 64 or experts % 16:
         return plain(master_gate, master_up, router_weight, router_gain, n)
     mine = lax.axis_index("shard")
     targets = jnp.stack([mine ^ d for d in range(n)]).astype(jnp.int32)
     masters = (master_gate, master_up)
     unit = experts // 16
-    lead = 5 * unit
+    lead = PLAN[LEAD][1] * unit
     plan = [(t, first * unit, count * unit) for t, first, count in PLAN]
 
     head = spread_direct(peaks(master_gate, 0, lead), n)
@@ -153,10 +155,10 @@
             scale, offset = head, first
         else:
             scale, offset = tail_scales[tensor], first - (lead if tensor == 0 else 0)
-        finals[tensor], *pieces = narrow(masters[tensor], scale, targets, first, count, offset, n, finals[tensor])
-        if k == LEAD - 1:
-            rest_gate = peaks(master_gate, lead, experts - lead, pieces)
-            rest_up = peaks(master_up, 0, experts, pieces)
+        finals[tensor], *pieces = narrow(masters[tensor], scale, targets, first, count, offset, n, 1, finals[tensor])
+        if k == LEAD - 2:
+            rest_gate = peaks(master_gate, lead, experts - lead, after=pieces)
+            rest_up = peaks(master_up, 0, experts, after=pieces)
             rest = spread_doubling(jnp.concatenate([rest_gate, rest_up], axis=0), n)
             tail_scales = [rest[: experts - lead], rest[experts - lead :]]
         sent.append([(d, swap(pieces[d - 1], "shard", n, d)) for d in range(n - 1, 0, -1)])

time: 445 us -> 424 us (0.953)
  waiting for transfers between devices: 273 us -> 260 us
  Pallas kernels: 88.1 us -> 81.2 us
    ppermute x34, waiting for transfers between devices: 273 us -> 260 us  [swap(): return lax.ppermute(value, axis, [(i, i ^ step) for i in range(size)])]
    pallas_call x3, Pallas kernels: 33.3 us -> 26 us  [peaks(): pl.pallas_call(peak_body, grid=(count // group,), in_specs=[pl.BlockSpec(...]
  transfers between devices with their start and end apart: 34 -> 34, of which waited for: 12 -> 11; matrix products, arithmetic and copies ran while one was open for 11% -> 12% of each run, Pallas kernels for 19% -> 18%
where the time goes in v2:
time: 424 us; the launch traced here: 422 us
  waiting for transfers between devices  260 us (61%)
  Pallas kernels  81.2 us (19%)
  local copies, waits for them, and re-layouts  49.2 us (12%)
  starting transfers between devices  27.2 us (6%)
    ppermute x34, waiting for transfers between devices, swap(): return lax.ppermute(value, axis, [(i, i ^ step) for i in range(size)])  260 us
    pallas_call x8, Pallas kernels, narrow(): pl.pallas_call(functools.partial(narrow_body, n), grid_spec=pltpu.Prefetc...  55.2 us
    dynamic_update_slice x24, local copies, waits for them, and re-layouts, shards(): lax.dynamic_update_slice(finals[tensor], piece, (first, (mine ^ d) * rows...  39.6 us
    ppermute x34, starting transfers between devices, swap(): return lax.ppermute(value, axis, [(i, i ^ step) for i in range(size)])  27.2 us
    pallas_call x3, Pallas kernels, peaks(): pl.pallas_call(peak_body, grid=(count // group,), in_specs=[pl.BlockSpec(...  26 us
  transfers between devices with their start and end apart: 34, of which 11 were waited for; matrix products, arithmetic and copies ran while one was open for 12% of the time, Pallas kernels for 18%

profile of v2, /device:TPU:0, one launch (start us, length us, event | category | flops | bytes accessed | tf_op | source)
XLA Modules:
  0.0 422.0 jit_solution(15005555547209412764)
XLA Ops:
  0.7 4.3 %peaks.3 = f32[4,1,1024]{2,1,0:T(1,128)} custom-call(f32[16,512,1024]{2,1,0:T(8,128)} %refs_3_.12), custom_call_target="tpu_custom_call" | custom-call | tf_op jit(solution)/shard_map/peaks/pallas_call | solution.py:27
  5.4 2.5 collective-permute-start.1
  8.1 1.8 collective-permute-start.29
  11.3 1.4 maximum_maximum_fusion.refs_4_.refs_5_.refs_6_.refs_7_
  12.6 3.2 narrow.8
  15.9 4.0 narrow.9
  19.9 9.5 %peaks.4 = f32[12,1,1024]{2,1,0:T(1,128)} custom-call(f32[16,512,1024]{2,1,0:T(8,128)} %refs_3_.12, bf16[2,512,256]{2,1,0:T(8,128)(2,1)} %get-tuple-element.38.refs_1_, bf16[2,512,256]{2,1,0:T(8,128)(2,1)} %get-tuple-element.39.refs_2_, bf16[2,512,256]{2,1,0:T(8,128)(2,1)} %get-tuple-element.40.refs_3_), custom_call_target="tpu_custom_call" | custom-call | tf_op jit(solution)/shard_map/peaks/pallas_call | solution.py:27
  29.4 12.2 %peaks.5 = f32[16,1,1024]{2,1,0:T(1,128)} custom-call(f32[16,512,1024]{2,1,0:T(8,128)} %refs_3_.15, bf16[2,512,256]{2,1,0:T(8,128)(2,1)} %get-tuple-element.38.refs_1_, bf16[2,512,256]{2,1,0:T(8,128)(2,1)} %get-tuple-element.39.refs_2_, bf16[2,512,256]{2,1,0:T(8,128)(2,1)} %get-tuple-element.40.refs_3_), custom_call_target="tpu_custom_call" | custom-call | tf_op jit(solution)/shard_map/peaks/pallas_call | solution.py:27
  46.2 1.7 collective-permute-start.31
  47.9 2.6 collective-permute-start.32
  51.0 3.3 narrow.10
  55.4 1.4 collective-permute-start.7
  56.8 1.4 collective-permute-start.12
  58.9 5.9 %narrow.11 = (bf16[16,2048,256]{2,1,0:T(8,128)(2,1)}, bf16[3,512,256]{2,1,0:T(8,128)(2,1)}, bf16[3,512,256]{2,1,0:T(8,128)(2,1)}, bf16[3,512,256]{2,1,0:T(8,128)(2,1)}) custom-call(s32[4]{0:T(128)} %pad_add_fusion.targets, f32[16,512,1024]{2,1,0:T(8,128)} %refs_3_.12, f32[16,512,1024]{2,1,0:T(8,128)} %refs_3_.12, ...), custom_call_target="tpu_custom_call", output_to_operand_aliasing={{0}: (9, {})} | custom-call | tf_op jit(solution)/shard_map/narrow/pallas_call | solution.py:62
  66.4 1.3 collective-permute-start.13
  67.7 2.8 collective-permute-done.12
  72.3 11.3 %narrow.13 = (bf16[16,2048,256]{2,1,0:T(8,128)(2,1)}, bf16[8,512,256]{2,1,0:T(8,128)(2,1)}, bf16[8,512,256]{2,1,0:T(8,128)(2,1)}, bf16[8,512,256]{2,1,0:T(8,128)(2,1)}) custom-call(s32[4]{0:T(128)} %pad_add_fusion.targets, f32[16,512,1024]{2,1,0:T(8,128)} %refs_3_.15, f32[16,512,1024]{2,1,0:T(8,128)} %refs_3_.15, f32[16,512,1024]{2,1,0:T(8,128)} %refs_3_.15, ...), custom_call_target="tpu_custom_call" | custom-call | tf_op jit(solution)/shard_map/narrow/pallas_call | solution.py:62
  83.7 3.9 collective-permute-done.13
  89.4 10.8 %narrow.14 = (bf16[16,2048,256]{2,1,0:T(8,128)(2,1)}, bf16[7,512,256]{2,1,0:T(8,128)(2,1)}, bf16[7,512,256]{2,1,0:T(8,128)(2,1)}, bf16[7,512,256]{2,1,0:T(8,128)(2,1)}) custom-call(s32[4]{0:T(128)} %pad_add_fusion.targets, f32[16,512,1024]{2,1,0:T(8,128)} %refs_3_.15, f32[16,512,1024]{2,1,0:T(8,128)} %refs_3_.15, ...), custom_call_target="tpu_custom_call", output_to_operand_aliasing={{0}: (9, {})} | custom-call | tf_op jit(solution)/shard_map/narrow/pallas_call | solution.py:62
  103.8 1.5 constant_dynamic-update-slice_fusion.2
  105.3 55.2 %collective-permute-done.15 = bf16[3,512,256]{2,1,0:T(8,128)(2,1)S(1)} collective-permute-done((bf16[3,512,256]{2,1,0:T(8,128)(2,1)}, bf16[3,512,256]{2,1,0:T(8,128)(2,1)S(1)}, u32[]{:S(2)}, u32[]{:S(2)}) %collective-permute-start.15) | collective-permute-done | bytes 786464 | tf_op jit(solution)/shard_map/ppermute | solution.py:17
  162.2 1.5 constant_dynamic-update-slice_fusion
  163.7 13.2 %narrow.12 = (bf16[16,2048,256]{2,1,0:T(8,128)(2,1)}, bf16[9,512,256]{2,1,0:T(8,128)(2,1)}, bf16[9,512,256]{2,1,0:T(8,128)(2,1)}, bf16[9,512,256]{2,1,0:T(8,128)(2,1)}) custom-call(s32[4]{0:T(128)} %pad_add_fusion.targets, f32[16,512,1024]{2,1,0:T(8,128)} %refs_3_.12, f32[16,512,1024]{2,1,0:T(8,128)} %refs_3_.12, ...), custom_call_target="tpu_custom_call", output_to_operand_aliasing={{0}: (9, {})} | custom-call | tf_op jit(solution)/shard_map/narrow/pallas_call | solution.py:62
  176.9 3.4 narrow.15
  182.3 1.7 constant_dynamic-update-slice_fusion.29
  183.9 38.5 %collective-permute-done.16 = bf16[3,512,256]{2,1,0:T(8,128)(2,1)} collective-permute-done((bf16[3,512,256]{2,1,0:T(8,128)(2,1)}, bf16[3,512,256]{2,1,0:T(8,128)(2,1)}, u32[]{:S(2)}, u32[]{:S(2)}) %collective-permute-start.16) | collective-permute-done | bytes 786464 | tf_op jit(solution)/shard_map/ppermute | solution.py:17
  223.0 1.7 constant_dynamic-update-slice_fusion.28
  224.7 1.7 constant_dynamic-update-slice_fusion.27
  228.7 1.9 constant_dynamic-update-slice_fusion.25
  231.0 1.9 constant_dynamic-update-slice_fusion.24
  233.9 1.7 constant_dynamic-update-slice_fusion.23
  235.6 1.7 constant_dynamic-update-slice_fusion.22
  237.2 1.7 constant_dynamic-update-slice_fusion.21
  238.9 2.1 constant_dynamic-update-slice_fusion.20
  241.9 2.1 constant_dynamic-update-slice_fusion.18
  243.9 3.0 constant_dynamic-update-slice_fusion.14
  247.0 1.5 constant_dynamic-update-slice_fusion.13
  248.4 3.0 constant_dynamic-update-slice_fusion.12
  251.5 13.2 %collective-permute-done.24 = bf16[7,512,256]{2,1,0:T(8,128)(2,1)S(1)} collective-permute-done((bf16[7,512,256]{2,1,0:T(8,128)(2,1)}, bf16[7,512,256]{2,1,0:T(8,128)(2,1)S(1)}, u32[]{:S(2)}, u32[]{:S(2)}) %collective-permute-start.24) | collective-permute-done | bytes 1835040 | tf_op jit(solution)/shard_map/ppermute | solution.py:17
  264.9 2.8 constant_dynamic-update-slice_fusion.11
  267.8 1.3 constant_dynamic-update-slice_fusion.10
  269.9 34.6 %collective-permute-done.25 = bf16[7,512,256]{2,1,0:T(8,128)(2,1)S(1)} collective-permute-done((bf16[7,512,256]{2,1,0:T(8,128)(2,1)}, bf16[7,512,256]{2,1,0:T(8,128)(2,1)S(1)}, u32[]{:S(2)}, u32[]{:S(2)}) %collective-permute-start.25) | collective-permute-done | bytes 1835040 | tf_op jit(solution)/shard_map/ppermute | solution.py:17
  305.5 1.3 constant_dynamic-update-slice_fusion.9
  307.5 103.3 %collective-permute-done.27 = bf16[1,512,256]{2,1,0:T(8,128)(2,1)S(1)} collective-permute-done((bf16[1,512,256]{2,1,0:T(8,128)(2,1)S(1)}, bf16[1,512,256]{2,1,0:T(8,128)(2,1)S(1)}, u32[]{:S(2)}, u32[]{:S(2)}) %collective-permute-start.27) | collective-permute-done | bytes 262176 | tf_op jit(solution)/shard_map/ppermute | solution.py:17
  411.5 5.1 %collective-permute-done.28 = bf16[1,512,256]{2,1,0:T(8,128)(2,1)S(1)} collective-permute-done((bf16[1,512,256]{2,1,0:T(8,128)(2,1)S(1)}, bf16[1,512,256]{2,1,0:T(8,128)(2,1)S(1)}, u32[]{:S(2)}, u32[]{:S(2)}) %collective-permute-start.28) | collective-permute-done | bytes 262176 | tf_op jit(solution)/shard_map/ppermute | solution.py:17
  417.3 1.6 constant_dynamic-update-slice_fusion.17
  418.9 1.6 constant_dynamic-update-slice_fusion.16
  420.5 1.6 constant_dynamic-update-slice_fusion.15
  (123 shorter events, 31.0 us)
Async XLA Ops:
  0.6 7.4 %copy-start.17 = (f32[512,16]{0,1:T(8,128)S(1)}, f32[512,16]{0,1:T(8,128)}, u32[]{:S(2)}) copy-start(f32[512,16]{0,1:T(8,128)} %param.6) | copy-start | bytes 98308
  0.6 7.4 %copy-start.18 = (f32[512]{0:T(512)S(1)}, f32[512]{0:T(512)}, u32[]{:S(2)}) copy-start(f32[512]{0:T(512)} %param.7) | copy-start | bytes 6148
  4.9 5.5 %collective-permute-start.2 = (f32[4,1,1024]{2,1,0:T(1,128)}, f32[4,1,1024]{2,1,0:T(1,128)S(1)}, u32[]{:S(2)}, u32[]{:S(2)}) collective-permute-start(f32[4,1,1024]{2,1,0:T(1,128)} %peaks.3), channel_id=1, source_target_pairs={{0,1},{1,0},{2,3},{3,2},{4,5},{5,4},{6,7},{7,6},{8,9},{9,8},{10,11... | collective-permute-start | bytes 49160 | tf_op jit(solution)/shard_map/ppermute | solution.py:17
  5.4 5.0 %collective-permute-start.1 = (f32[4,1,1024]{2,1,0:T(1,128)}, f32[4,1,1024]{2,1,0:T(1,128)S(1)}, u32[]{:S(2)}, u32[]{:S(2)}) collective-permute-start(f32[4,1,1024]{2,1,0:T(1,128)} %peaks.3), channel_id=1, source_target_pairs={{0,2},{1,3},{2,0},{3,1},{4,6},{5,7},{6,4},{7,5},{8,10},{9,11},{10,... | collective-permute-start | bytes 49160 | tf_op jit(solution)/shard_map/ppermute | solution.py:17
  7.9 3.4 collective-permute-start
  8.1 35.0 %collective-permute-start.29 = (bf16[16,512]{1,0:T(8,128)(2,1)S(1)}, bf16[16,512]{1,0:T(8,128)(2,1)S(1)}, u32[]{:S(2)}, u32[]{:S(2)}) collective-permute-start(bf16[16,512]{1,0:T(8,128)(2,1)S(1)} %get-tuple-element.70), channel_id=1, source_target_pairs={{0,2},{1,3},{2,0},{3,1},{4,6},{5,7},{6,4},{7,5},{8,10},{9,11},{10,... | collective-permute-start | bytes 49160 | tf_op jit(solution)/shard_map/ppermute | solution.py:17
  29.4 12.2 %copy-start.7 = (f32[12,1,1024]{2,1,0:T(1,128)S(1)}, f32[12,1,1024]{2,1,0:T(1,128)}, u32[]{:S(2)}) copy-start(f32[12,1,1024]{2,1,0:T(1,128)} %peaks.4) | copy-start | bytes 147460
  42.5 2.1 collective-permute-start.3
  42.8 22.0 %collective-permute-start.5 = (bf16[1,512,256]{2,1,0:T(8,128)(2,1)}, bf16[1,512,256]{2,1,0:T(8,128)(2,1)S(1)}, u32[]{:S(2)}, u32[]{:S(2)}) collective-permute-start(bf16[1,512,256]{2,1,0:T(8,128)(2,1)} %get-tuple-element.45), channel_id=1, source_target_pairs={{0,1},{1,0},{2,3},{3,2},{4,5},{5,4},{6,7},{7,6},{8,9},{9,8},{10,11... | collective-permute-start | bytes 786440 | tf_op jit(solution)/shard_map/ppermute | solution.py:17
  43.1 1.5 collective-permute-start.30
  45.6 11.1 %collective-permute-start.4 = (f32[28,1,1024]{2,1,0:T(1,128)S(1)}, f32[28,1,1024]{2,1,0:T(1,128)S(1)}, u32[]{:S(2)}, u32[]{:S(2)}) collective-permute-start(f32[28,1,1024]{2,1,0:T(1,128)S(1)} %fusion.2), channel_id=1, source_target_pairs={{0,2},{1,3},{2,0},{3,1},{4,6},{5,7},{6,4},{7,5},{8,10},{9,11},{10,... | collective-permute-start | bytes 344072 | tf_op jit(solution)/shard_map/ppermute | solution.py:17
  46.2 8.2 %copy-start.13 = (bf16[16,2048]{1,0:T(8,128)(2,1)}, bf16[16,2048]{1,0:T(8,128)(2,1)S(1)}, u32[]{:S(2)}) copy-start(bf16[16,2048]{1,0:T(8,128)(2,1)S(1)} %slice_dynamic-update-slice_fusion) | copy-start | bytes 196612
  46.2 4.4 %collective-permute-start.31 = (bf16[16,2048]{1,0:T(8,128)(2,1)S(1)}, bf16[16,2048]{1,0:T(8,128)(2,1)S(1)}, u32[]{:S(2)}, u32[]{:S(2)}) collective-permute-start(bf16[16,2048]{1,0:T(8,128)(2,1)S(1)} %slice_dynamic-update-slice_fusion), channel_id=1, source_target_pairs={{0,4},{4,0},{8,12},{12,8},{1,5},{5,1},{9,13},{13,9},{2,6},{6,2},{1... | collective-permute-start | bytes 196616 | tf_op jit(solution)/shard_map/ppermute | solution.py:17
  47.9 7.5 %collective-permute-start.32 = (bf16[16,2048]{1,0:T(8,128)(2,1)S(1)}, bf16[16,2048]{1,0:T(8,128)(2,1)S(1)}, u32[]{:S(2)}, u32[]{:S(2)}) collective-permute-start(bf16[16,2048]{1,0:T(8,128)(2,1)S(1)} %slice_dynamic-update-slice_fusion), channel_id=1, source_target_pairs={{0,8},{4,12},{8,0},{12,4},{1,9},{5,13},{9,1},{13,5},{2,10},{6,14},... | collective-permute-start | bytes 196616 | tf_op jit(solution)/shard_map/ppermute | solution.py:17
  50.5 6.3 %collective-permute-start.33 = (bf16[16,2048]{1,0:T(8,128)(2,1)S(1)}, bf16[16,2048]{1,0:T(8,128)(2,1)S(1)}, u32[]{:S(2)}, u32[]{:S(2)}) collective-permute-start(bf16[16,2048]{1,0:T(8,128)(2,1)S(1)} %slice_dynamic-update-slice_fusion), channel_id=1, source_target_pairs={{0,12},{4,8},{8,4},{12,0},{1,13},{5,9},{9,5},{13,1},{2,14},{6,10},... | collective-permute-start | bytes 196616 | tf_op jit(solution)/shard_map/ppermute | solution.py:17
  50.6 15.0 %collective-permute-start.6 = (bf16[1,512,256]{2,1,0:T(8,128)(2,1)}, bf16[1,512,256]{2,1,0:T(8,128)(2,1)}, u32[]{:S(2)}, u32[]{:S(2)}) collective-permute-start(bf16[1,512,256]{2,1,0:T(8,128)(2,1)} %get-tuple-element.46), channel_id=1, source_target_pairs={{0,3},{1,2},{2,1},{3,0},{4,7},{5,6},{6,5},{7,4},{8,11},{9,10},{10,... | collective-permute-start | bytes 786440 | tf_op jit(solution)/shard_map/ppermute | solution.py:17
  55.4 10.2 %collective-permute-start.7 = (bf16[1,512,256]{2,1,0:T(8,128)(2,1)S(1)}, bf16[1,512,256]{2,1,0:T(8,128)(2,1)S(1)}, u32[]{:S(2)}, u32[]{:S(2)}) collective-permute-start(bf16[1,512,256]{2,1,0:T(8,128)(2,1)S(1)} %copy-done.21), channel_id=1, source_target_pairs={{0,2},{1,3},{2,0},{3,1},{4,6},{5,7},{6,4},{7,5},{8,10},{9,11},{10,... | collective-permute-start | bytes 786440 | tf_op jit(solution)/shard_map/ppermute | solution.py:17
  56.8 9.7 %collective-permute-start.11 = (bf16[1,512,256]{2,1,0:T(8,128)(2,1)}, bf16[1,512,256]{2,1,0:T(8,128)(2,1)S(1)}, u32[]{:S(2)}, u32[]{:S(2)}) collective-permute-start(bf16[1,512,256]{2,1,0:T(8,128)(2,1)} %get-tuple-element.48), channel_id=1, source_target_pairs={{0,1},{1,0},{2,3},{3,2},{4,5},{5,4},{6,7},{7,6},{8,9},{9,8},{10,11... | collective-permute-start | bytes 786440 | tf_op jit(solution)/shard_map/ppermute | solution.py:17
  56.8 13.8 %collective-permute-start.12 = (bf16[1,512,256]{2,1,0:T(8,128)(2,1)}, bf16[1,512,256]{2,1,0:T(8,128)(2,1)S(1)}, u32[]{:S(2)}, u32[]{:S(2)}) collective-permute-start(bf16[1,512,256]{2,1,0:T(8,128)(2,1)} %get-tuple-element.49), channel_id=1, source_target_pairs={{0,3},{1,2},{2,1},{3,0},{4,7},{5,6},{6,5},{7,4},{8,11},{9,10},{10,... | collective-permute-start | bytes 786440 | tf_op jit(solution)/shard_map/ppermute | solution.py:17
  58.9 11.6 %copy-start.2 = (bf16[2,512,256]{2,1,0:T(8,128)(2,1)S(1)}, bf16[2,512,256]{2,1,0:T(8,128)(2,1)}, u32[]{:S(2)}) copy-start(bf16[2,512,256]{2,1,0:T(8,128)(2,1)} %get-tuple-element.39.refs_2_) | copy-start | bytes 1572868
  64.8 36.8 %collective-permute-start.14 = (bf16[3,512,256]{2,1,0:T(8,128)(2,1)}, bf16[3,512,256]{2,1,0:T(8,128)(2,1)}, u32[]{:S(2)}, u32[]{:S(2)}) collective-permute-start(bf16[3,512,256]{2,1,0:T(8,128)(2,1)} %get-tuple-element.51), channel_id=1, source_target_pairs={{0,1},{1,0},{2,3},{3,2},{4,5},{5,4},{6,7},{7,6},{8,9},{9,8},{10,11... | collective-permute-start | bytes 2359304 | tf_op jit(solution)/shard_map/ppermute | solution.py:17
  65.5 22.0 %collective-permute-start.8 = (bf16[2,512,256]{2,1,0:T(8,128)(2,1)S(1)}, bf16[2,512,256]{2,1,0:T(8,128)(2,1)S(1)}, u32[]{:S(2)}, u32[]{:S(2)}) collective-permute-start(bf16[2,512,256]{2,1,0:T(8,128)(2,1)S(1)} %copy-done.4), channel_id=1, source_target_pairs={{0,1},{1,0},{2,3},{3,2},{4,5},{5,4},{6,7},{7,6},{8,9},{9,8},{10,11... | collective-permute-start | bytes 1572872 | tf_op jit(solution)/shard_map/ppermute | solution.py:17
  65.6 18.1 %copy-start.11 = (bf16[1,512,256]{2,1,0:T(8,128)(2,1)}, bf16[1,512,256]{2,1,0:T(8,128)(2,1)S(1)}, u32[]{:S(2)}) copy-start(bf16[1,512,256]{2,1,0:T(8,128)(2,1)S(1)} %collective-permute-done.7) | copy-start | bytes 786436
  65.6 34.6 %collective-permute-start.9 = (bf16[2,512,256]{2,1,0:T(8,128)(2,1)S(1)}, bf16[2,512,256]{2,1,0:T(8,128)(2,1)}, u32[]{:S(2)}, u32[]{:S(2)}) collective-permute-start(bf16[2,512,256]{2,1,0:T(8,128)(2,1)S(1)} %copy-done.3), channel_id=1, source_target_pairs={{0,3},{1,2},{2,1},{3,0},{4,7},{5,6},{6,5},{7,4},{8,11},{9,10},{10,... | collective-permute-start | bytes 1572872 | tf_op jit(solution)/shard_map/ppermute | solution.py:17
  66.4 17.2 %copy-start.9 = (bf16[1,512,256]{2,1,0:T(8,128)(2,1)}, bf16[1,512,256]{2,1,0:T(8,128)(2,1)S(1)}, u32[]{:S(2)}) copy-start(bf16[1,512,256]{2,1,0:T(8,128)(2,1)S(1)} %collective-permute-done.11) | copy-start | bytes 786436
  66.4 21.1 %collective-permute-start.13 = (bf16[1,512,256]{2,1,0:T(8,128)(2,1)}, bf16[1,512,256]{2,1,0:T(8,128)(2,1)S(1)}, u32[]{:S(2)}, u32[]{:S(2)}) collective-permute-start(bf16[1,512,256]{2,1,0:T(8,128)(2,1)} %get-tuple-element.50), channel_id=1, source_target_pairs={{0,2},{1,3},{2,0},{3,1},{4,6},{5,7},{6,4},{7,5},{8,10},{9,11},{10,... | collective-permute-start | bytes 786440 | tf_op jit(solution)/shard_map/ppermute | solution.py:17
  70.5 13.2 %copy-start.10 = (bf16[1,512,256]{2,1,0:T(8,128)(2,1)}, bf16[1,512,256]{2,1,0:T(8,128)(2,1)S(1)}, u32[]{:S(2)}) copy-start(bf16[1,512,256]{2,1,0:T(8,128)(2,1)S(1)} %collective-permute-done.12) | copy-start | bytes 786436
  70.5 30.1 %collective-permute-start.10 = (bf16[2,512,256]{2,1,0:T(8,128)(2,1)S(1)}, bf16[2,512,256]{2,1,0:T(8,128)(2,1)}, u32[]{:S(2)}, u32[]{:S(2)}) collective-permute-start(bf16[2,512,256]{2,1,0:T(8,128)(2,1)S(1)} %copy-done.2), channel_id=1, source_target_pairs={{0,2},{1,3},{2,0},{3,1},{4,6},{5,7},{6,4},{7,5},{8,10},{9,11},{10,... | collective-permute-start | bytes 1572872 | tf_op jit(solution)/shard_map/ppermute | solution.py:17
  87.6 12.6 %copy-start.12 = (bf16[1,512,256]{2,1,0:T(8,128)(2,1)}, bf16[1,512,256]{2,1,0:T(8,128)(2,1)S(1)}, u32[]{:S(2)}) copy-start(bf16[1,512,256]{2,1,0:T(8,128)(2,1)S(1)} %collective-permute-done.13) | copy-start | bytes 786436
  87.6 139.2 %collective-permute-start.20 = (bf16[8,512,256]{2,1,0:T(8,128)(2,1)}, bf16[8,512,256]{2,1,0:T(8,128)(2,1)}, u32[]{:S(2)}, u32[]{:S(2)}) collective-permute-start(bf16[8,512,256]{2,1,0:T(8,128)(2,1)} %get-tuple-element.60), channel_id=1, source_target_pairs={{0,1},{1,0},{2,3},{3,2},{4,5},{5,4},{6,7},{7,6},{8,9},{9,8},{10,11... | collective-permute-start | bytes 6291464 | tf_op jit(solution)/shard_map/ppermute | solution.py:17
  88.4 142.2 %collective-permute-start.21 = (bf16[8,512,256]{2,1,0:T(8,128)(2,1)}, bf16[8,512,256]{2,1,0:T(8,128)(2,1)S(1)}, u32[]{:S(2)}, u32[]{:S(2)}) collective-permute-start(bf16[8,512,256]{2,1,0:T(8,128)(2,1)} %get-tuple-element.61), channel_id=1, source_target_pairs={{0,3},{1,2},{2,1},{3,0},{4,7},{5,6},{6,5},{7,4},{8,11},{9,10},{10,... | collective-permute-start | bytes 6291464 | tf_op jit(solution)/shard_map/ppermute | solution.py:17
  89.3 13.8 %copy-start.14 = (bf16[16,2048]{1,0:T(8,128)(2,1)S(1)}, bf16[16,2048]{1,0:T(8,128)(2,1)}, u32[]{:S(2)}) copy-start(bf16[16,2048]{1,0:T(8,128)(2,1)} %copy-done.13) | copy-start | bytes 196612
  100.2 126.2 %collective-permute-start.23 = (bf16[7,512,256]{2,1,0:T(8,128)(2,1)}, bf16[7,512,256]{2,1,0:T(8,128)(2,1)}, u32[]{:S(2)}, u32[]{:S(2)}) collective-permute-start(bf16[7,512,256]{2,1,0:T(8,128)(2,1)} %get-tuple-element.63), channel_id=1, source_target_pairs={{0,1},{1,0},{2,3},{3,2},{4,5},{5,4},{6,7},{7,6},{8,9},{9,8},{10,11... | collective-permute-start | bytes 5505032 | tf_op jit(solution)/shard_map/ppermute | solution.py:17
  100.7 59.7 %collective-permute-start.15 = (bf16[3,512,256]{2,1,0:T(8,128)(2,1)}, bf16[3,512,256]{2,1,0:T(8,128)(2,1)S(1)}, u32[]{:S(2)}, u32[]{:S(2)}) collective-permute-start(bf16[3,512,256]{2,1,0:T(8,128)(2,1)} %get-tuple-element.52), channel_id=1, source_target_pairs={{0,3},{1,2},{2,1},{3,0},{4,7},{5,6},{6,5},{7,4},{8,11},{9,10},{10,... | collective-permute-start | bytes 2359304 | tf_op jit(solution)/shard_map/ppermute | solution.py:17
  101.6 131.2 %collective-permute-start.22 = (bf16[8,512,256]{2,1,0:T(8,128)(2,1)}, bf16[8,512,256]{2,1,0:T(8,128)(2,1)}, u32[]{:S(2)}, u32[]{:S(2)}) collective-permute-start(bf16[8,512,256]{2,1,0:T(8,128)(2,1)} %get-tuple-element.62), channel_id=1, source_target_pairs={{0,2},{1,3},{2,0},{3,1},{4,6},{5,7},{6,4},{7,5},{8,10},{9,11},{10,... | collective-permute-start | bytes 6291464 | tf_op jit(solution)/shard_map/ppermute | solution.py:17
  160.4 62.0 %collective-permute-start.16 = (bf16[3,512,256]{2,1,0:T(8,128)(2,1)}, bf16[3,512,256]{2,1,0:T(8,128)(2,1)}, u32[]{:S(2)}, u32[]{:S(2)}) collective-permute-start(bf16[3,512,256]{2,1,0:T(8,128)(2,1)} %get-tuple-element.53), channel_id=1, source_target_pairs={{0,2},{1,3},{2,0},{3,1},{4,6},{5,7},{6,4},{7,5},{8,10},{9,11},{10,... | collective-permute-start | bytes 2359304 | tf_op jit(solution)/shard_map/ppermute | solution.py:17
  176.9 51.0 %copy-start.6 = (bf16[2,512,256]{2,1,0:T(8,128)(2,1)S(1)}, bf16[2,512,256]{2,1,0:T(8,128)(2,1)}, u32[]{:S(2)}) copy-start(bf16[2,512,256]{2,1,0:T(8,128)(2,1)} %copy-done.5) | copy-start | bytes 1572868
  180.3 84.5 %copy-start.22 = (bf16[1,512,256]{2,1,0:T(8,128)(2,1)S(1)}, bf16[1,512,256]{2,1,0:T(8,128)(2,1)}, u32[]{:S(2)}) copy-start(bf16[1,512,256]{2,1,0:T(8,128)(2,1)} %get-tuple-element.66) | copy-start | bytes 786436
  180.3 88.9 %copy-start.20 = (bf16[1,512,256]{2,1,0:T(8,128)(2,1)S(1)}, bf16[1,512,256]{2,1,0:T(8,128)(2,1)}, u32[]{:S(2)}) copy-start(bf16[1,512,256]{2,1,0:T(8,128)(2,1)} %get-tuple-element.67) | copy-start | bytes 786436
  180.3 124.2 %copy-start.19 = (bf16[1,512,256]{2,1,0:T(8,128)(2,1)S(1)}, bf16[1,512,256]{2,1,0:T(8,128)(2,1)}, u32[]{:S(2)}) copy-start(bf16[1,512,256]{2,1,0:T(8,128)(2,1)} %get-tuple-element.68) | copy-start | bytes 786436
  222.4 42.3 %collective-permute-start.24 = (bf16[7,512,256]{2,1,0:T(8,128)(2,1)}, bf16[7,512,256]{2,1,0:T(8,128)(2,1)S(1)}, u32[]{:S(2)}, u32[]{:S(2)}) collective-permute-start(bf16[7,512,256]{2,1,0:T(8,128)(2,1)} %get-tuple-element.64), channel_id=1, source_target_pairs={{0,3},{1,2},{2,1},{3,0},{4,7},{5,6},{6,5},{7,4},{8,11},{9,10},{10,... | collective-permute-start | bytes 5505032 | tf_op jit(solution)/shard_map/ppermute | solution.py:17
  226.4 190.9 %collective-permute-start.17 = (bf16[9,512,256]{2,1,0:T(8,128)(2,1)}, bf16[9,512,256]{2,1,0:T(8,128)(2,1)S(1)}, u32[]{:S(2)}, u32[]{:S(2)}) collective-permute-start(bf16[9,512,256]{2,1,0:T(8,128)(2,1)} %get-tuple-element.54), channel_id=1, source_target_pairs={{0,1},{1,0},{2,3},{3,2},{4,5},{5,4},{6,7},{7,6},{8,9},{9,8},{10,11... | collective-permute-start | bytes 7077896 | tf_op jit(solution)/shard_map/ppermute | solution.py:17
  226.8 77.7 %collective-permute-start.25 = (bf16[7,512,256]{2,1,0:T(8,128)(2,1)}, bf16[7,512,256]{2,1,0:T(8,128)(2,1)S(1)}, u32[]{:S(2)}, u32[]{:S(2)}) collective-permute-start(bf16[7,512,256]{2,1,0:T(8,128)(2,1)} %get-tuple-element.65), channel_id=1, source_target_pairs={{0,2},{1,3},{2,0},{3,1},{4,6},{5,7},{6,4},{7,5},{8,10},{9,11},{10,... | collective-permute-start | bytes 5505032 | tf_op jit(solution)/shard_map/ppermute | solution.py:17
  230.6 188.3 %collective-permute-start.18 = (bf16[9,512,256]{2,1,0:T(8,128)(2,1)}, bf16[9,512,256]{2,1,0:T(8,128)(2,1)S(1)}, u32[]{:S(2)}, u32[]{:S(2)}) collective-permute-start(bf16[9,512,256]{2,1,0:T(8,128)(2,1)} %get-tuple-element.55), channel_id=1, source_target_pairs={{0,3},{1,2},{2,1},{3,0},{4,7},{5,6},{6,5},{7,4},{8,11},{9,10},{10,... | collective-permute-start | bytes 7077896 | tf_op jit(solution)/shard_map/ppermute | solution.py:17
  232.8 187.6 %collective-permute-start.19 = (bf16[9,512,256]{2,1,0:T(8,128)(2,1)}, bf16[9,512,256]{2,1,0:T(8,128)(2,1)S(1)}, u32[]{:S(2)}, u32[]{:S(2)}) collective-permute-start(bf16[9,512,256]{2,1,0:T(8,128)(2,1)} %get-tuple-element.56), channel_id=1, source_target_pairs={{0,2},{1,3},{2,0},{3,1},{4,6},{5,7},{6,4},{7,5},{8,10},{9,11},{10,... | collective-permute-start | bytes 7077896 | tf_op jit(solution)/shard_map/ppermute | solution.py:17
  264.7 4.4 %collective-permute-start.26 = (bf16[1,512,256]{2,1,0:T(8,128)(2,1)S(1)}, bf16[1,512,256]{2,1,0:T(8,128)(2,1)S(1)}, u32[]{:S(2)}, u32[]{:S(2)}) collective-permute-start(bf16[1,512,256]{2,1,0:T(8,128)(2,1)S(1)} %copy-done.22), channel_id=1, source_target_pairs={{0,1},{1,0},{2,3},{3,2},{4,5},{5,4},{6,7},{7,6},{8,9},{9,8},{10,11... | collective-permute-start | bytes 786440 | tf_op jit(solution)/shard_map/ppermute | solution.py:17
  269.1 141.6 %collective-permute-start.27 = (bf16[1,512,256]{2,1,0:T(8,128)(2,1)S(1)}, bf16[1,512,256]{2,1,0:T(8,128)(2,1)S(1)}, u32[]{:S(2)}, u32[]{:S(2)}) collective-permute-start(bf16[1,512,256]{2,1,0:T(8,128)(2,1)S(1)} %copy-done.20), channel_id=1, source_target_pairs={{0,3},{1,2},{2,1},{3,0},{4,7},{5,6},{6,5},{7,4},{8,11},{9,10},{10,... | collective-permute-start | bytes 786440 | tf_op jit(solution)/shard_map/ppermute | solution.py:17
  304.4 112.2 %collective-permute-start.28 = (bf16[1,512,256]{2,1,0:T(8,128)(2,1)S(1)}, bf16[1,512,256]{2,1,0:T(8,128)(2,1)S(1)}, u32[]{:S(2)}, u32[]{:S(2)}) collective-permute-start(bf16[1,512,256]{2,1,0:T(8,128)(2,1)S(1)} %copy-done.19), channel_id=1, source_target_pairs={{0,2},{1,3},{2,0},{3,1},{4,6},{5,7},{6,4},{7,5},{8,10},{9,11},{10,... | collective-permute-start | bytes 786440 | tf_op jit(solution)/shard_map/ppermute | solution.py:17
  (9 other events, 32.0 us)
